TPU v7x, 256 devices: a whole 4x4x8 slice. The times are simulated.
256 devices in a mesh: dp: 8 (over z), expert: 32 (over x, y, core).
Axes of the slice: x: 4, y: 4, z: 8, core: 2. Of those that a mesh axis runs over, the one named last changes fastest.
Arguments:
- tokens: bfloat16 [2048, 7168], P('expert'), may hold values from -6 to 6
- routes: int32 [2048, 8], P('expert'), may hold values from 0 to 31, all different within a row; in each aligned block of 64 rows (0 to 63, 64 to 127, ...) at most 20 rows name the same one
- route_weight: int32 [2048, 8], P('expert'), may hold values from 1 to 4096
- w_gate: bfloat16 [32, 7168, 2048], P('expert', None, 'dp'), may hold values from -0.0625 to 0.0625
- w_up: bfloat16 [32, 7168, 2048], P('expert', None, 'dp'), may hold values from -0.0625 to 0.0625
- w_down: bfloat16 [32, 2048, 7168], P('expert', 'dp'), may hold values from -0.125 to 0.125
- prev_inputs: bfloat16 [8, 32, 64, 7168], P('dp', 'expert'), may hold values from -6 to 6
Outputs:
- mixed: bfloat16 [2048, 7168], P('expert', 'dp')
- hessian: float32 [7168, 32, 128], P('dp', 'expert')
Inputs may be any that keep to these rules, and one draw needn't show every extreme that they name: `routes`: in each aligned block of 64 rows (the rows of one index of expert) no expert is named more than 20 times, a bound that some block reaches; the 8 experts of a token differ.
All inputs are finite; a program needn't handle non-finite values.
Results may differ from a plain program's by a relative error of at most 0.014.
Values may be sent and summed in bfloat16 or wider, within the bound.
A program may use at most 128 MiB of HBM per device.

v0:
```python
import jax
import jax.numpy as jnp
from jax import lax
from jax.sharding import PartitionSpec as P

HESS_COLS = 128


def split_up(value, dim, length):
    before, after = (value.shape[:dim], value.shape[dim + 1 :])
    return jnp.moveaxis(value.reshape(*before, length, -1, *after), dim, 0)


def summed_on_arrival(value, axis, dim):
    blocks = split_up(value, dim, lax.axis_size(axis))
    arrived = lax.all_to_all(blocks, axis, split_axis=0, concat_axis=0, tiled=True)
    return arrived.astype(jnp.float32).sum(axis=0)


def route_slots(flat_ids, experts_all):
    onehot = (flat_ids[:, None] == jnp.arange(experts_all, dtype=jnp.int32)[None, :]).astype(
        jnp.int32
    )
    earlier = jnp.cumsum(onehot, axis=0) - onehot
    return jnp.sum(earlier * onehot, axis=1)


def combine_rows(back, places, shares, tok_dev, top):
    columns = back.shape[-1]
    rows = back.reshape(-1, columns)[places]
    weighted = rows.astype(jnp.float32) * shares.reshape(-1, 1)
    return jnp.sum(weighted.reshape(tok_dev, top, columns), axis=1)


def shards(tokens, routes, route_weight, w_gate, w_up, w_down, prev_inputs):
    tok_dev, top = routes.shape
    exp_dev = w_gate.shape[0]
    width = tokens.shape[1]
    n_expert = lax.axis_size("expert")
    n_dp = lax.axis_size("dp")
    experts_all = exp_dev * n_expert
    capacity = min(tok_dev, tok_dev * top * 5 // (4 * experts_all))
    col_width = width // n_dp
    flat_ids = routes.reshape(-1)
    slots = route_slots(flat_ids, experts_all)
    places = flat_ids * capacity + slots
    weight_counts = route_weight.astype(jnp.float32)
    shares = 2.5 * weight_counts / jnp.sum(weight_counts, axis=1, keepdims=True)
    picks = jnp.arange(experts_all * capacity, dtype=jnp.int32)[:, None] == places[None, :]
    placing = jnp.any(picks.reshape(experts_all * capacity, tok_dev, top), axis=2).astype(
        jnp.bfloat16
    )
    my_cols = lax.dynamic_slice_in_dim(tokens, lax.axis_index("dp") * col_width, col_width, 1)
    outgoing = jnp.dot(placing, my_cols, preferred_element_type=jnp.float32).astype(jnp.bfloat16)
    outgoing = outgoing.reshape(experts_all, capacity, col_width)
    arrived = lax.all_to_all(outgoing, "expert", split_axis=0, concat_axis=0, tiled=True)
    arrived = arrived.reshape(n_expert, exp_dev, capacity, col_width)
    piece = lax.all_gather(arrived, "dp", axis=3, tiled=True)
    gate_add = jnp.einsum("sjcd,jdf->sjcf", piece, w_gate, preferred_element_type=jnp.float32)
    up_add = jnp.einsum("sjcd,jdf->sjcf", piece, w_up, preferred_element_type=jnp.float32)
    history = prev_inputs.reshape(prev_inputs.shape[1], prev_inputs.shape[2], width)
    head_cols = history[:, :, :HESS_COLS]
    gram_scale = 2.0 / (n_dp * history.shape[1])
    hessian = lax.psum_scatter(
        (
            jnp.einsum("jrd,jrh->djh", history, head_cols, preferred_element_type=jnp.float32)
            * gram_scale
        ).astype(jnp.bfloat16),
        "dp",
        scatter_dimension=0,
        tiled=True,
    ).astype(jnp.float32)
    hidden = (jax.nn.silu(gate_add) * up_add).astype(jnp.bfloat16)
    partial_out = jnp.einsum("sjcf,jfd->sjcd", hidden, w_down, preferred_element_type=jnp.float32)
    partial_out = partial_out.astype(jnp.bfloat16)
    back = lax.all_to_all(
        partial_out.reshape(experts_all, capacity, width),
        "expert",
        split_axis=0,
        concat_axis=0,
        tiled=True,
    )
    own_sum = combine_rows(back, places, shares, tok_dev, top)
    mixed = summed_on_arrival(own_sum.astype(jnp.bfloat16), "dp", 1)
    return (mixed.astype(jnp.bfloat16), hessian)


def solution(mesh):
    placed = (
        P("expert", None),
        P("expert", None),
        P("expert", None),
        P("expert", None, "dp"),
        P("expert", None, "dp"),
        P("expert", "dp", None),
        P("dp", "expert", None, None),
    )
    return jax.shard_map(
        shards,
        mesh=mesh,
        in_specs=placed,
        out_specs=(P("expert", "dp"), P("dp", "expert", None)),
        check_vma=False,
    )
```

profile of v0, /device:TPU:8, one launch (start us, length us, event | category | flops | bytes accessed | tf_op | source)
XLA Modules:
  0.0 429.0 jit_solution(2899087094357470166)
XLA Ops:
  7.2 0.8 copy.38
  8.1 0.1 eq.44
  8.3 1.2 reduce-window.6
  9.4 0.2 slice_reduce_fusion
  9.7 0.1 fusion.28
  9.8 0.1 reduce_sum.44
  9.9 0.5 fusion.8
  10.4 0.5 convolution_convert_fusion.1
  10.9 0.3 reshape.127
  11.2 26.5 %all_to_all.15 = bf16[32,20,896]{2,1,0:T(8,128)(2,1)S(1)} all-to-all(bf16[32,20,896]{2,1,0:T(8,128)(2,1)S(1)} %reshape.127), channel_id=1, replica_groups=mesh['dp'=8,'expert'=32] {'expert'}, dimensions={0} | all-to-all | bytes 2293760 | tf_op jit(solution)/shard_map/all_to_all | solution.py:56
  37.7 1.1 copy.42
  38.9 102.2 %all-gather.3.cloned.1.call-done = bf16[32,20,7168]{2,0,1:T(8,128)(2,1)} async-done(((bf16[32,20,896]{2,0,1:T(8,128)(2,1)}), bf16[32,20,7168]{2,0,1:T(8,128)(2,1)}) %all-gather.3.cloned.1.call-update) | async-done | bytes 9175056 | tf_op jit(solution)/shard_map/all_gather | solution.py:58
  141.1 7.3 %fusion.9 = f32[32,1,20,256]{3,0,2,1:T(8,128)S(1)} fusion(bf16[32,20,7168]{2,0,1:T(8,128)(2,1)} %all-gather.3.cloned.1.call-done, bf16[1,7168,256]{2,1,0:T(8,128)(2,1)} %param.10), kind=kOutput, calls=%fused_computation.15 | convolution fusion | flops 2348810240 | bytes 13500416 | tf_op jit(solution)/shard_map/sjcd,jdf->sjcf/dot_general | solution.py:59
  148.5 1.0 copy-done.6
  149.4 2.5 fusion.21
  152.0 6.1 %convolution_convert_fusion = bf16[32,20,7168]{2,0,1:T(8,128)(2,1)} fusion(bf16[32,20,256]{2,0,1:T(8,128)(2,1)S(1)} %fusion.21, bf16[1,256,7168]{2,1,0:T(8,128)(2,1)S(1)} %copy-done.2), kind=kOutput, calls=%fused_computation.3 | convolution fusion | flops 2353397760 | bytes 13172736 | tf_op jit(solution)/shard_map/sjcf,jfd->sjcd/dot_general | solution.py:74
  158.1 13.0 %copy.43 = bf16[32,20,7168]{2,1,0:T(8,128)(2,1)} copy(bf16[32,20,7168]{2,0,1:T(8,128)(2,1)} %convolution_convert_fusion) | data formatting | bytes 18350080 | tf_op jit(solution)/shard_map/convert_element_type | solution.py:75
  171.0 7.6 %all-to-all-start.1 = ((bf16[32,20,7168]{2,1,0:T(8,128)(2,1)}), bf16[32,20,7168]{2,1,0:T(8,128)(2,1)}, u32[]{:S(2)}, u32[]{:S(2)}) async-start(bf16[32,20,7168]{2,1,0:T(8,128)(2,1)} %copy.43), calls=%async_computation.1 | async-start | bytes 22020096 | tf_op jit(solution)/shard_map/all_to_all | solution.py:76
  178.7 0.7 fusion.2
  179.4 2.3 copy.49
  181.7 0.1 mul.62
  182.0 167.4 %all-to-all-done.1 = bf16[32,20,7168]{2,1,0:T(8,128)(2,1)} async-done(((bf16[32,20,7168]{2,1,0:T(8,128)(2,1)}), bf16[32,20,7168]{2,1,0:T(8,128)(2,1)}, u32[]{:S(2)}, u32[]{:S(2)}) %all-to-all-start.1) | async-done | bytes 9175072 | tf_op jit(solution)/shard_map/all_to_all | solution.py:76
  349.4 13.3 %reshape.134 = bf16[640,7168]{1,0:T(8,128)(2,1)} reshape(bf16[32,20,7168]{2,1,0:T(8,128)(2,1)} %all-to-all-done.1) | data formatting | bytes 18350080 | tf_op jit(solution)/shard_map/reshape | solution.py:30
  362.7 18.6 %gather_fusion = bf16[512,7168]{1,0:T(8,128)(2,1)} fusion(bf16[640,7168]{1,0:T(8,128)(2,1)} %reshape.134, s32[1024]{0:T(1024)S(1)} %pad_clamp_fusion), kind=kCustom, calls=%fused_computation | custom fusion | bytes 14682112 | tf_op jit(solution)/shard_map/gather | solution.py:30
  381.3 8.9 %fusion = bf16[64,7168]{1,0:T(8,128)(2,1)S(1)} fusion(bf16[512,7168]{1,0:T(8,128)(2,1)} %gather_fusion, f32[64,8]{1,0:T(8,128)S(1)} %copy.44), kind=kLoop, calls=%fused_computation.2 | loop fusion | flops 10551296 | bytes 8259584 | tf_op jit(solution)/shard_map/reduce_sum | solution.py:32
  390.2 0.1 copy.52
  390.4 1.1 copy.45
  391.5 4.3 %all-to-all-start.2 = ((bf16[8,64,896]{2,1,0:T(8,128)(2,1)}), bf16[8,64,896]{2,1,0:T(8,128)(2,1)S(1)}, u32[]{:S(2)}, u32[]{:S(2)}) async-start(bf16[8,64,896]{2,1,0:T(8,128)(2,1)} %copy.45), calls=%async_computation.2 | async-start | bytes 1835008 | tf_op jit(solution)/shard_map/all_to_all | solution.py:16
  395.8 1.1 copy.50
  396.9 1.1 copy.46
  398.0 23.4 %all-to-all-done.2 = bf16[8,64,896]{2,1,0:T(8,128)(2,1)S(1)} async-done(((bf16[8,64,896]{2,1,0:T(8,128)(2,1)}), bf16[8,64,896]{2,1,0:T(8,128)(2,1)S(1)}, u32[]{:S(2)}, u32[]{:S(2)}) %all-to-all-start.2) | async-done | bytes 917536 | tf_op jit(solution)/shard_map/all_to_all | solution.py:16
  421.4 0.8 reduce_sum.48
  (29 shorter events, 0.5 us)
Async XLA Ops:
  7.2 3.2 copy-start
  7.2 133.9 %all-gather.3.cloned.1.call-start = ((), (), s32[]{:S(2)}) async-start(), calls=%async_computation.4 | async-start | bytes 10321920 | tf_op jit(solution)/shard_map/all_gather | solution.py:58
  141.1 7.3 %copy-start.5 = (bf16[32,20,7168]{2,0,1:T(8,128)(2,1)S(1)}, bf16[32,20,7168]{2,0,1:T(8,128)(2,1)}, u32[]{:S(2)}) copy-start(bf16[32,20,7168]{2,0,1:T(8,128)(2,1)} %all-gather.3.cloned.1.call-done) | copy-start | bytes 27525124
  141.1 8.3 %copy-start.6 = (bf16[1,7168,256]{2,1,0:T(8,128)(2,1)S(1)}, bf16[1,7168,256]{2,1,0:T(8,128)(2,1)}, u32[]{:S(2)}) copy-start(bf16[1,7168,256]{2,1,0:T(8,128)(2,1)} %param.11) | copy-start | bytes 11010052
  149.4 2.5 copy-start.2
  171.0 7.6 %copy-start.3 = (bf16[1,1,64,7168]{3,2,1,0:T(8,128)(2,1)S(1)}, bf16[1,1,64,7168]{3,2,1,0:T(8,128)(2,1)}, u32[]{:S(2)}) copy-start(bf16[1,1,64,7168]{3,2,1,0:T(8,128)(2,1)} %param.13) | copy-start | bytes 2752516
  171.0 178.3 %all-to-all-start.1 = ((bf16[32,20,7168]{2,1,0:T(8,128)(2,1)}), bf16[32,20,7168]{2,1,0:T(8,128)(2,1)}, u32[]{:S(2)}, u32[]{:S(2)}) async-start(bf16[32,20,7168]{2,1,0:T(8,128)(2,1)} %copy.43), calls=%async_computation.1 | async-start | bytes 22020096 | tf_op jit(solution)/shard_map/all_to_all | solution.py:76
  178.6 217.2 %reduce-scatter.4.cloned.1.call-start = ((), (), s32[]{:S(2)}) async-start(), calls=%async_computation.5 | async-start | bytes 2064384
  178.7 3.1 copy-start.4
  390.2 32.0 %copy-start.1 = (bf16[64,7168]{1,0:T(8,128)(2,1)S(1)}, bf16[64,7168]{1,0:T(8,128)(2,1)}, u32[]{:S(2)}) copy-start(bf16[64,7168]{1,0:T(8,128)(2,1)} %param.7) | copy-start | bytes 2752516
  391.5 29.9 %all-to-all-start.2 = ((bf16[8,64,896]{2,1,0:T(8,128)(2,1)}), bf16[8,64,896]{2,1,0:T(8,128)(2,1)S(1)}, u32[]{:S(2)}, u32[]{:S(2)}) async-start(bf16[8,64,896]{2,1,0:T(8,128)(2,1)} %copy.45), calls=%async_computation.2 | async-start | bytes 1835008 | tf_op jit(solution)/shard_map/all_to_all | solution.py:16
Sparse Core Ops, SparseCore 0:
  39.0 102.0 all-gather.2
  182.0 40.2 reduce-scatter.3
where the time goes:
time: 431 us; the launch traced here: 429 us
  waiting for transfers between devices  293 us (68%)
  local copies, waits for them, and re-layouts  54.5 us (13%)
  blocking collectives  26.5 us (6%)
  matrix products  17.1 us (4%)
  between operations  14.2 us (3%)
  starting transfers between devices  12 us (3%)
  other arithmetic  11.6 us (3%)
    all_to_all x1, waiting for transfers between devices, shards(): lax.all_to_all(partial_out.reshape(experts_all, capacity, width), 'expert...  167 us
    all_gather x1, waiting for transfers between devices, shards(): piece = lax.all_gather(arrived, 'dp', axis=3, tiled=True)  102 us
    all_to_all x1, blocking collectives, shards(): lax.all_to_all(outgoing, 'expert', split_axis=0, concat_axis=0, tiled=True)  26.5 us
    all_to_all x1, waiting for transfers between devices, summed_on_arrival(): lax.all_to_all(blocks, axis, split_axis=0, concat_axis=0, tiled=True)  23.4 us
    gather x1, local copies, waits for them, and re-layouts, combine_rows(): rows = back.reshape(-1, columns)[places]  18.6 us
    reshape x1, local copies, waits for them, and re-layouts, combine_rows(): rows = back.reshape(-1, columns)[places]  13.3 us
    convert_element_type x1, local copies, waits for them, and re-layouts, shards(): partial_out = partial_out.astype(jnp.bfloat16)  13 us
    reduce_sum x1, other arithmetic, combine_rows(): return jnp.sum(weighted.reshape(tok_dev, top, columns), axis=1)  8.91 us
  transfers between devices with their start and end apart: 4, of which 3 were waited for; matrix products, arithmetic and copies ran while one was open for 11% of the time, Pallas kernels for 0%

commit v1 on v0

v1 whole, which is shorter than its diff:
```python
import functools

import jax
import jax.numpy as jnp
from jax import lax
from jax.experimental import pallas as pl
from jax.experimental.pallas import tpu as pltpu
from jax.sharding import PartitionSpec as P

HESS_COLS = 128
PARTS = 2
BOTH = ("dp", "expert")


def experts_kernel(groups, t_ref, wg_ref, wu_ref, wd_ref, share_ref, out_ref, gate, up, hidden):
    step = pl.program_id(0)

    @pl.when(step < groups)
    def _():
        rows = t_ref[0]
        more_gate = jnp.dot(rows, wg_ref[...], preferred_element_type=jnp.float32)
        more_up = jnp.dot(rows, wu_ref[...], preferred_element_type=jnp.float32)

        @pl.when(step == 0)
        def _():
            gate[...] = more_gate
            up[...] = more_up

        @pl.when(step > 0)
        def _():
            gate[...] += more_gate
            up[...] += more_up

    @pl.when(step == groups - 1)
    def _():
        value = gate[...]
        hidden[...] = (value / (1.0 + jnp.exp(-value)) * up[...]).astype(jnp.bfloat16)

    @pl.when(step >= groups)
    def _():
        part = jnp.dot(hidden[...], wd_ref[...], preferred_element_type=jnp.float32)
        part = part.astype(jnp.bfloat16).astype(jnp.float32)
        out_ref[...] = (part * share_ref[...]).astype(jnp.bfloat16)


def experts(gathered, w_gate, w_up, w_down, share):
    groups, rows, cols = gathered.shape
    ff = w_gate.shape[1]
    first = lambda i: jnp.minimum(i, groups - 1)
    second = lambda i: jnp.maximum(i - groups, 0)
    return pl.pallas_call(
        functools.partial(experts_kernel, groups),
        grid=(2 * groups,),
        out_shape=jax.ShapeDtypeStruct((rows, groups * cols), jnp.bfloat16),
        in_specs=[
            pl.BlockSpec((1, rows, cols), lambda i: (first(i), 0, 0)),
            pl.BlockSpec((cols, ff), lambda i: (first(i), 0)),
            pl.BlockSpec((cols, ff), lambda i: (first(i), 0)),
            pl.BlockSpec((ff, cols), lambda i: (0, second(i))),
            pl.BlockSpec((rows, 1), lambda i: (0, 0)),
        ],
        out_specs=pl.BlockSpec((rows, cols), lambda i: (0, second(i))),
        scratch_shapes=[
            pltpu.VMEM((rows, ff), jnp.float32),
            pltpu.VMEM((rows, ff), jnp.float32),
            pltpu.VMEM((rows, ff), jnp.bfloat16),
        ],
        compiler_params=pltpu.CompilerParams(
            dimension_semantics=("arbitrary",), vmem_limit_bytes=48 * 2**20
        ),
        cost_estimate=pl.CostEstimate(
            flops=6 * rows * groups * cols * ff,
            bytes_accessed=2 * (2 * groups * rows * cols + 3 * groups * cols * ff),
            transcendentals=rows * ff,
        ),
    )(gathered, w_gate, w_up, w_down, share)


def shards(tokens, routes, route_weight, w_gate, w_up, w_down, prev_inputs):
    tok_dev, top = routes.shape
    width = tokens.shape[1]
    n_expert = lax.axis_size("expert")
    n_dp = lax.axis_size("dp")
    col_width = width // n_dp
    tok_part = tok_dev // PARTS
    my_cols = lax.dynamic_slice_in_dim(tokens, lax.axis_index("dp") * col_width, col_width, 1)
    gathered = []
    for p in range(PARTS):
        block = my_cols[p * tok_part : (p + 1) * tok_part]
        whole = lax.all_gather(block, BOTH, axis=0, tiled=False)
        gathered.append(whole.reshape(n_dp, n_expert * tok_part, col_width))

    weight_counts = route_weight.astype(jnp.float32)
    shares = 2.5 * weight_counts / jnp.sum(weight_counts, axis=1, keepdims=True)
    named = jnp.arange(n_expert, dtype=jnp.int32)[:, None, None] == routes[None]
    by_expert = jnp.sum(jnp.where(named, shares[None], 0.0), axis=2)
    mine = lax.all_to_all(by_expert, "expert", split_axis=0, concat_axis=0, tiled=True)

    history = prev_inputs.reshape(prev_inputs.shape[2], width)
    head = lax.all_gather(history[:, :HESS_COLS], "dp", axis=0, tiled=True)
    pieces = jnp.moveaxis(history.reshape(-1, n_dp, col_width), 1, 0)
    pieces = lax.all_to_all(pieces, "dp", split_axis=0, concat_axis=0, tiled=True)
    stacked = pieces.reshape(-1, col_width)
    hessian = jnp.einsum("rd,rh->dh", stacked, head, preferred_element_type=jnp.float32)
    hessian = (hessian * (2.0 / stacked.shape[0]))[:, None, :]

    mixed = []
    for p in range(PARTS):
        share = mine[:, p * tok_part : (p + 1) * tok_part].reshape(-1, 1)
        out = experts(gathered[p], w_gate[0], w_up[0], w_down[0], share)
        own = lax.psum_scatter(out, "expert", scatter_dimension=0, tiled=True)
        own = jnp.moveaxis(own.reshape(tok_part, n_dp, col_width), 1, 0)
        mixed.append(lax.psum_scatter(own, "dp", scatter_dimension=0, tiled=True)[0])
    return (jnp.concatenate(mixed, axis=0), hessian)


def solution(mesh):
    placed = (
        P("expert", None),
        P("expert", None),
        P("expert", None),
        P("expert", None, "dp"),
        P("expert", None, "dp"),
        P("expert", "dp", None),
        P("dp", "expert", None, None),
    )
    return jax.shard_map(
        shards,
        mesh=mesh,
        in_specs=placed,
        out_specs=(P("expert", "dp"), P("dp", "expert", None)),
        check_vma=False,
    )
```

time: 431 us -> 590 us (1.37)
  waiting for transfers between devices: 293 us -> 463 us
  Pallas kernels: 0 us -> 48.9 us
  local copies, waits for them, and re-layouts: 54.5 us -> 12.9 us
  matrix products: 17.1 us -> 1.21 us
  blocking collectives: 26.5 us -> 39.6 us
  other arithmetic: 11.6 us -> 3.63 us
  starting transfers between devices: 12 us -> 4.61 us
    reduce_scatter x0 -> x4, waiting for transfers between devices: none -> 253 us  [the longest x2 204 us: shards(): own = lax.psum_scatter(out, 'expert', scatter_dimension=0, tiled=True)]
    all_to_all x2 -> x1, waiting for transfers between devices: 191 us -> 0.01 us  [shards(): lax.all_to_all(pieces, 'dp', split_axis=0, concat_axis=0, tiled=True)]
    all_gather x1 -> x2, waiting for transfers between devices: 102 us -> 209 us  [shards(): whole = lax.all_gather(block, BOTH, axis=0, tiled=False)]
    pallas_call x0 -> x2, Pallas kernels: none -> 48.9 us  [experts(): pl.pallas_call(functools.partial(experts_kernel, groups), grid=(2 * group...]
    all_gather x0 -> x1, blocking collectives: none -> 26.1 us  [shards(): head = lax.all_gather(history[:, :HESS_COLS], 'dp', axis=0, tiled=True)]
    gather x1 -> x0, local copies, waits for them, and re-layouts: 18.6 us -> none  [combine_rows(): rows = back.reshape(-1, columns)[places]]
    dot_general x5 -> x1, matrix products: 17.1 us -> 1.21 us  [shards(): jnp.einsum('rd,rh->dh', stacked, head, preferred_element_type=jnp.float32)]
    all_to_all x1, blocking collectives: 26.5 us -> 13.5 us  [shards(): lax.all_to_all(by_expert, 'expert', split_axis=0, concat_axis=0, tiled=True)]
  transfers between devices with their start and end apart: 4 -> 7, of which waited for: 3 -> 6; matrix products, arithmetic and copies ran while one was open for 11% -> 2% of each run, Pallas kernels for 0% -> 8%
where the time goes in v1:
time: 590 us; the launch traced here: 588 us
  waiting for transfers between devices  463 us (78%)
  Pallas kernels  48.9 us (8%)
  blocking collectives  39.6 us (7%)
  between operations  14.2 us (2%)
  local copies, waits for them, and re-layouts  12.9 us (2%)
    all_gather x2, waiting for transfers between devices, shards(): whole = lax.all_gather(block, BOTH, axis=0, tiled=False)  209 us
    reduce_scatter x2, waiting for transfers between devices, shards(): own = lax.psum_scatter(out, 'expert', scatter_dimension=0, tiled=True)  204 us
    reduce_scatter x2, waiting for transfers between devices, shards(): lax.psum_scatter(own, 'dp', scatter_dimension=0, tiled=True)[0]  49 us
    pallas_call x2, Pallas kernels, experts(): pl.pallas_call(functools.partial(experts_kernel, groups), grid=(2 * group...  48.9 us
    all_gather x1, blocking collectives, shards(): head = lax.all_gather(history[:, :HESS_COLS], 'dp', axis=0, tiled=True)  26.1 us
    all_to_all x1, blocking collectives, shards(): lax.all_to_all(by_expert, 'expert', split_axis=0, concat_axis=0, tiled=True)  13.5 us
  transfers between devices with their start and end apart: 7, of which 6 were waited for; matrix products, arithmetic and copies ran while one was open for 2% of the time, Pallas kernels for 8%

profile of v1, /device:TPU:8, one launch (start us, length us, event | category | flops | bytes accessed | tf_op | source)
XLA Modules:
  0.0 588.2 jit_solution(1897874779142593459)
XLA Ops:
  7.2 0.0 all-gather.7.cloned.1.call-start
  7.2 1.5 constant_dynamic-slice_fusion
  8.7 0.0 all-gather.5.cloned.1.call-start
  8.8 0.7 all-gather.5.cloned.1.call-update
  9.5 0.7 convert_reduce_fusion
  10.2 0.7 multiply_divide_fusion
  10.9 0.7 select_reduce_fusion
  11.7 13.5 %all_to_all.17 = f32[32,1,64]{2,1,0:T(1,128)S(1)} all-to-all(f32[32,1,64]{2,1,0:T(1,128)S(1)} %bitcast.50), channel_id=1, replica_groups=mesh['dp'=8,'expert'=32] {'expert'}, dimensions={0} | all-to-all | bytes 16384 | tf_op jit(solution)/shard_map/all_to_all | solution.py:97
  25.2 0.1 fusion
  25.3 0.5 reshape.46.share_ref
  25.8 112.0 %all-gather.7.cloned.1.call-done = bf16[8192,896]{1,0:T(8,128)(2,1)} async-done(((bf16[32,896]{1,0:T(8,128)(2,1)}), bf16[8192,896]{1,0:T(8,128)(2,1)}) %all-gather.7.cloned.1.call-update) | async-done | bytes 14680080 | tf_op jit(solution)/shard_map/all_gather | solution.py:90
  137.8 2.0 copy-done
  139.9 24.2 %shard_map.87 = bf16[1024,7168]{1,0:T(8,128)(2,1)} custom-call(bf16[8,1024,896]{2,1,0:T(8,128)(2,1)} %bitcast.54, bf16[7168,256]{1,0:T(8,128)(2,1)S(1)} %bitcast.38, bf16[7168,256]{1,0:T(8,128)(2,1)} %bitcast.55, bf16[256,7168]{1,0:T(8,128)(2,1)} %bitcast.57, f32[1024,1]{1,0:T(8,128)S(1)} %reshape.46.share_ref), custom_call_target="tpu_custom_call" | custom-call | flops 11274289152 | bytes 40370176 | tf_op jit(solution)/shard_map/pallas_call | solution.py:51
  164.1 0.0 reduce-scatter.5.cloned.1.call-start
  164.1 0.5 reshape.45.share_ref
  164.7 97.5 %all-gather.5.cloned.1.call-done = bf16[8192,896]{1,0:T(8,128)(2,1)} async-done(((bf16[32,896]{1,0:T(8,128)(2,1)}), bf16[8192,896]{1,0:T(8,128)(2,1)}) %all-gather.5.cloned.1.call-update) | async-done | bytes 14680080 | tf_op jit(solution)/shard_map/all_gather | solution.py:90
  262.1 2.0 copy-done.1
  264.2 24.6 %shard_map.86 = bf16[1024,7168]{1,0:T(8,128)(2,1)} custom-call(bf16[8,1024,896]{2,1,0:T(8,128)(2,1)} %bitcast.53, bf16[7168,256]{1,0:T(8,128)(2,1)S(1)} %bitcast.39, bf16[7168,256]{1,0:T(8,128)(2,1)} %bitcast.56, bf16[256,7168]{1,0:T(8,128)(2,1)} %bitcast.58, f32[1024,1]{1,0:T(8,128)S(1)} %reshape.45.share_ref), custom_call_target="tpu_custom_call" | custom-call | flops 11274289152 | bytes 40370176 | tf_op jit(solution)/shard_map/pallas_call | solution.py:51
  288.8 1.2 copy-done.2
  290.1 0.1 copy.46
  290.2 1.1 copy.42
  291.3 4.4 all-to-all-start.1
  295.8 85.1 %reduce-scatter.9.cloned.1.call-done = bf16[32,7168]{1,0:T(8,128)(2,1)} async-done(((bf16[1024,7168]{1,0:T(8,128)(2,1)}), bf16[32,7168]{1,0:T(8,128)(2,1)}) %reduce-scatter.9.cloned.1.call-update) | async-done | bytes 458768 | tf_op jit(solution)/shard_map/reduce_scatter | solution.py:111
  380.9 1.8 copy.49
  382.7 0.0 reduce-scatter.7.cloned.1.call-start
  382.8 118.9 %reduce-scatter.5.cloned.1.call-done = bf16[32,7168]{1,0:T(8,128)(2,1)} async-done(((bf16[1024,7168]{1,0:T(8,128)(2,1)}), bf16[32,7168]{1,0:T(8,128)(2,1)}) %reduce-scatter.5.cloned.1.call-update) | async-done | bytes 458768 | tf_op jit(solution)/shard_map/reduce_scatter | solution.py:111
  501.7 1.8 copy.50
  503.6 26.1 %all_gather.19 = bf16[512,128]{1,0:T(8,128)(2,1)S(1)} all-gather(bf16[64,128]{1,0:T(8,128)(2,1)S(1)} %slice.22), channel_id=1, replica_groups=mesh['dp'=8,'expert'=32] {'dp'}, dimensions={0}, use_global_device_ids=true | all-gather | bytes 147456 | tf_op jit(solution)/shard_map/all_gather | solution.py:100
  529.7 1.2 convolution_multiply_fusion
  530.9 10.5 %reduce-scatter.11.cloned.1.call-done = bf16[1,32,896]{2,1,0:T(8,128)(2,1)} async-done(((bf16[8,32,896]{2,1,0:T(8,128)(2,1)}), bf16[1,32,896]{2,1,0:T(8,128)(2,1)}) %reduce-scatter.11.cloned.1.call-update) | async-done | bytes 57360 | tf_op jit(solution)/shard_map/reduce_scatter | solution.py:113
  541.4 38.5 %reduce-scatter.7.cloned.1.call-done = bf16[1,32,896]{2,1,0:T(8,128)(2,1)} async-done(((bf16[8,32,896]{2,1,0:T(8,128)(2,1)}), bf16[1,32,896]{2,1,0:T(8,128)(2,1)}) %reduce-scatter.7.cloned.1.call-update) | async-done | bytes 57360 | tf_op jit(solution)/shard_map/reduce_scatter | solution.py:113
  579.9 1.5 pad_maximum_fusion
  (12 shorter events, 0.2 us)
Async XLA Ops:
  7.2 130.7 %all-gather.7.cloned.1.call-start = ((), (), s32[]{:S(2)}) async-start(), calls=%async_computation.11 | async-start | bytes 14737408 | tf_op jit(solution)/shard_map/all_gather | solution.py:90
  8.7 253.4 %all-gather.5.cloned.1.call-start = ((), (), s32[]{:S(2)}) async-start(), calls=%async_computation.10 | async-start | bytes 14737408 | tf_op jit(solution)/shard_map/all_gather | solution.py:90
  9.5 371.4 %reduce-scatter.9.cloned.1.call-start = ((), (), s32[]{:S(2)}) async-start(), calls=%async_computation.8 | async-start | bytes 15138816 | tf_op jit(solution)/shard_map/reduce_scatter | solution.py:111
  137.8 2.0 copy-start
  164.1 337.6 %reduce-scatter.5.cloned.1.call-start = ((), (), s32[]{:S(2)}) async-start(), calls=%async_computation.6 | async-start | bytes 15138816 | tf_op jit(solution)/shard_map/reduce_scatter | solution.py:111
  262.1 2.0 copy-start.1
  288.8 1.2 copy-start.2
  291.3 238.3 %all-to-all-start.1 = ((bf16[8,64,896]{2,1,0:T(8,128)(2,1)}), bf16[8,64,896]{2,1,0:T(8,128)(2,1)S(1)}, u32[]{:S(2)}, u32[]{:S(2)}) async-start(bf16[8,64,896]{2,1,0:T(8,128)(2,1)} %copy.42), calls=%async_computation.5 | async-start | bytes 1835008 | tf_op jit(solution)/shard_map/all_to_all | solution.py:102
  295.7 245.7 %reduce-scatter.11.cloned.1.call-start = ((), (), s32[]{:S(2)}) async-start(), calls=%async_computation.9 | async-start | bytes 516096 | tf_op jit(solution)/shard_map/reduce_scatter | solution.py:113
  382.7 197.2 %reduce-scatter.7.cloned.1.call-start = ((), (), s32[]{:S(2)}) async-start(), calls=%async_computation.7 | async-start | bytes 516096 | tf_op jit(solution)/shard_map/reduce_scatter | solution.py:113
Sparse Core Ops, SparseCore 0:
  12.1 125.6 all-gather.6
  142.0 120.1 all-gather.4
  266.3 114.4 reduce-scatter.8
  384.9 116.7 reduce-scatter.4
  504.1 37.2 reduce-scatter.10
  543.7 36.0 reduce-scatter.6

commit v2 on v1

v2 whole, which is shorter than its diff:
```python
import functools

import jax
import jax.numpy as jnp
from jax import lax
from jax.experimental import pallas as pl
from jax.experimental.pallas import tpu as pltpu
from jax.sharding import PartitionSpec as P

HESS_COLS = 128
SIDE = 4
CHIPS = SIDE * SIDE
UNITS = 56
SWAP_UNITS = 18
MESH = pl.DeviceIdType.MESH
BF16 = jnp.bfloat16
F32 = jnp.float32


class Place:
    def __init__(self):
        self.n_dp = lax.axis_size("dp")
        self.z = lax.axis_index("dp")
        e = lax.axis_index("expert")
        self.core = lax.rem(e, 2)
        chip = e // 2
        self.y = lax.rem(chip, SIDE)
        self.x = chip // SIDE

    def block(self, axis, first, second):
        dx, dy = (first, second) if axis == "x" else (second, first)
        return lax.rem(self.x + dx + SIDE, SIDE) * SIDE + lax.rem(self.y + dy + SIDE, SIDE)

    def device(self, dx=0, dy=0, dz=0):
        chip = self.block("x", dx, dy)
        return (lax.rem(self.z + dz + self.n_dp, self.n_dp), chip * 2 + self.core)

    def toward(self, axis, step):
        return self.device(dx=step) if axis == "x" else self.device(dy=step)

    def partner(self):
        chip = self.block("x", 0, 0)
        return (self.z, chip * 2 + 1 - self.core)


def greet(devices):
    barrier = pltpu.get_barrier_semaphore()
    for device in devices:
        pl.semaphore_signal(barrier, inc=1, device_id=device, device_id_type=MESH)
    pl.semaphore_wait(barrier, len(devices))


def remote(src, dst, send_sem, recv_sem, device):
    return pltpu.make_async_remote_copy(
        src_ref=src,
        dst_ref=dst,
        send_sem=send_sem,
        recv_sem=recv_sem,
        device_id=device,
        device_id_type=MESH,
    )


def take_turns(flows):
    flows = list(flows)
    while flows:
        left = []
        for flow in flows:
            try:
                next(flow)
                left.append(flow)
            except StopIteration:
                pass
        flows = left


def gather_kernel(
    tok_ref, share_ref, wg_ref, wu_ref, wd_ref,
    all_ref, shares_ref, wg2_ref, wu2_ref, wd2_ref,
    flow_send, flow_recv, z_send, z_recv, s_send, s_recv, w_send, w_recv, local_sem,
):
    here = Place()
    width = tok_ref.shape[1]
    unit = width // UNITS
    offsets = [(i, j) for i in range(SIDE) for j in range(SIDE) if (i, j) != (0, 0)]
    z_steps = (1, -1)
    greet([here.device(dx=i, dy=j) for i, j in offsets]
          + [here.device(dz=s) for s in z_steps] + [here.partner()])
    own = here.block("x", 0, 0)
    started = []

    def go(copy):
        copy.start()
        started.append(copy)
        return copy

    parity = lax.rem(here.z, 2)
    swap = SWAP_UNITS * unit
    swap_from = pl.multiple_of((1 - parity) * swap, unit)
    wanted_from = pl.multiple_of(parity * swap, unit)

    def flow(number, axis, other, start, span, swapped):
        half = span // 2
        whole = pl.ds(start, span)
        part_a, part_b = pl.ds(start, half), pl.ds(pl.multiple_of(start + half, unit), half)

        def send(t, rel, cols, along, step, local=False):
            block = here.block(axis, *rel)
            src = tok_ref.at[:, cols] if local else all_ref.at[block, :, cols]
            return go(remote(src, all_ref.at[block, :, cols], flow_send.at[number, t],
                             flow_recv.at[number, t], here.toward(along, step)))

        def across(rel, which):
            if not swapped:
                return
            block = here.block(axis, *rel)
            slot = (rel[0] % SIDE) * SIDE + rel[1] % SIDE
            for side in which:
                cols = (part_a, part_b)[side]
                ref = all_ref.at[block, :, cols]
                go(remote(ref, ref, z_send.at[side, slot], z_recv.at[side, slot],
                          here.device(dz=z_steps[side])))

        c = {}
        c[0] = send(0, (0, 0), whole, axis, 1, True)
        c[1] = send(1, (0, 0), whole, axis, -1, True)
        c[2] = send(2, (0, 0), whole, other, 1, True)
        c[3] = send(3, (0, 0), whole, other, -1, True)
        yield
        c[0].wait_recv()
        c[4] = send(4, (-1, 0), part_a, axis, 1)
        c[5] = send(5, (-1, 0), whole, other, 1)
        c[6] = send(6, (-1, 0), whole, other, -1)
        across((-1, 0), (0, 1))
        c[1].wait_recv()
        c[7] = send(7, (1, 0), part_b, axis, -1)
        c[8] = send(8, (1, 0), whole, other, 1)
        c[9] = send(9, (1, 0), whole, other, -1)
        across((1, 0), (0, 1))
        yield
        c[2].wait_recv()
        c[10] = send(10, (0, -1), part_a, other, 1)
        across((0, -1), (0, 1))
        c[3].wait_recv()
        c[11] = send(11, (0, 1), part_b, other, -1)
        across((0, 1), (0, 1))
        yield
        c[4].wait_recv()
        across((2, 0), (0,))
        c[7].wait_recv()
        across((2, 0), (1,))
        c[12] = send(12, (2, 0), whole, other, 1)
        c[13] = send(13, (2, 0), whole, other, -1)
        yield
        c[5].wait_recv()
        c[14] = send(14, (-1, -1), part_a, other, 1)
        across((-1, -1), (0, 1))
        c[6].wait_recv()
        c[15] = send(15, (-1, 1), part_b, other, -1)
        across((-1, 1), (0, 1))
        yield
        c[8].wait_recv()
        c[16] = send(16, (1, -1), part_a, other, 1)
        across((1, -1), (0, 1))
        c[9].wait_recv()
        c[17] = send(17, (1, 1), part_b, other, -1)
        across((1, 1), (0, 1))
        yield
        c[10].wait_recv()
        across((0, 2), (0,))
        c[11].wait_recv()
        across((0, 2), (1,))
        yield
        c[12].wait_recv()
        c[18] = send(18, (2, -1), part_a, other, 1)
        across((2, -1), (0, 1))
        c[13].wait_recv()
        c[19] = send(19, (2, 1), part_b, other, -1)
        across((2, 1), (0, 1))
        yield
        for t, rel, side in ((14, (-1, 2), 0), (15, (-1, 2), 1), (16, (1, 2), 0), (17, (1, 2), 1),
                             (18, (2, 2), 0), (19, (2, 2), 1)):
            c[t].wait_recv()
            across(rel, (side,))
        yield

    def extras():
        mine = pltpu.make_async_copy(tok_ref, all_ref.at[own], local_sem)
        mine.start()
        yield
        gifts = []
        for n, (i, j) in enumerate(offsets):
            gifts.append(go(remote(share_ref.at[here.block("x", i, j)], shares_ref.at[own],
                                   s_send.at[n], s_recv.at[n], here.device(dx=i, dy=j))))
        for n, (src, dst) in enumerate(((wg_ref, wg2_ref), (wu_ref, wu2_ref), (wd_ref, wd2_ref))):
            gifts.append(go(remote(src, dst, w_send.at[n], w_recv.at[n], here.partner())))
        shares_ref[own] = share_ref[own]
        for _ in range(6):
            yield
        for gift in gifts:
            gift.wait_recv()
        mine.wait()

    fixed = 2 * swap
    take_turns([
        flow(0, "x", "y", fixed, width - fixed, False),
        flow(1, "y", "x", swap_from, swap, True),
        extras(),
    ])
    half = swap // 2
    for side in (0, 1):
        cols = pl.ds(pl.multiple_of(wanted_from + side * half, unit), half)
        for i, j in offsets:
            ref = all_ref.at[here.block("y", i, j), :, cols]
            slot = i * SIDE + j
            remote(ref, ref, z_send.at[side, slot], z_recv.at[side, slot],
                   here.device(dz=z_steps[side])).wait_recv()
    for copy in started:
        copy.wait_send()


def gather_all(tokens, share, w_gate, w_up, w_down):
    rows, width = tokens.shape
    vmem, hbm = pl.BlockSpec(memory_space=pltpu.VMEM), pl.BlockSpec(memory_space=pl.ANY)
    dma = pltpu.SemaphoreType.DMA
    like = lambda a: jax.ShapeDtypeStruct(a.shape, a.dtype)
    return pl.pallas_call(
        gather_kernel,
        out_shape=[
            jax.ShapeDtypeStruct((CHIPS, rows, width), BF16),
            like(share), like(w_gate), like(w_up), like(w_down),
        ],
        in_specs=[vmem, vmem, hbm, hbm, hbm],
        out_specs=[hbm, vmem, hbm, hbm, hbm],
        scratch_shapes=[
            dma((2, 20)), dma((2, 20)), dma((2, CHIPS)), dma((2, CHIPS)),
            dma((CHIPS - 1,)), dma((CHIPS - 1,)), dma((3,)), dma((3,)), dma(()),
        ],
        compiler_params=pltpu.CompilerParams(
            collective_id=0, has_side_effects=True, vmem_limit_bytes=60 * 2**20
        ),
    )(tokens, share, w_gate, w_up, w_down)


def experts_kernel(
    steps, t_ref, ga_ref, ua_ref, gb_ref, ub_ref, da_ref, db_ref, share_ref, out_ref,
    sums, hidden,
):
    step = pl.program_id(0)

    @pl.when(step < steps)
    def _():
        rows = t_ref[...]
        for n, w_ref in enumerate((ga_ref, ua_ref, gb_ref, ub_ref)):
            more = jnp.dot(rows, w_ref[...], preferred_element_type=F32)

            @pl.when(step == 0)
            def _():
                sums[n] = more

            @pl.when(step > 0)
            def _():
                sums[n] += more

    @pl.when(step == steps - 1)
    def _():
        for n in range(2):
            gate = sums[2 * n]
            value = gate / (1.0 + jnp.exp(-gate)) * sums[2 * n + 1]
            hidden[n] = (value * share_ref[:, n : n + 1]).astype(BF16)

    @pl.when(step >= steps)
    def _():
        total = jnp.dot(hidden[0], da_ref[...], preferred_element_type=F32)
        total += jnp.dot(hidden[1], db_ref[...], preferred_element_type=F32)
        out_ref[...] = total.astype(BF16)


def experts(rows_all, own, other, share):
    rows, width = rows_all.shape
    ff = own[0].shape[1]
    steps = max(1, width // 1024)
    cols = width // steps
    first = lambda i: jnp.minimum(i, steps - 1)
    second = lambda i: jnp.maximum(i - steps, 0)
    up_spec = pl.BlockSpec((cols, ff), lambda i: (first(i), 0))
    down_spec = pl.BlockSpec((ff, cols), lambda i: (0, second(i)))
    return pl.pallas_call(
        functools.partial(experts_kernel, steps),
        grid=(2 * steps,),
        out_shape=jax.ShapeDtypeStruct((rows, width), BF16),
        in_specs=[
            pl.BlockSpec((rows, cols), lambda i: (0, first(i))),
            up_spec, up_spec, up_spec, up_spec, down_spec, down_spec,
            pl.BlockSpec((rows, 2), lambda i: (0, 0)),
        ],
        out_specs=pl.BlockSpec((rows, cols), lambda i: (0, second(i))),
        scratch_shapes=[pltpu.VMEM((4, rows, ff), F32), pltpu.VMEM((2, rows, ff), BF16)],
        compiler_params=pltpu.CompilerParams(
            dimension_semantics=("arbitrary",), vmem_limit_bytes=56 * 2**20
        ),
        cost_estimate=pl.CostEstimate(
            flops=12 * rows * width * ff,
            bytes_accessed=4 * rows * width + 12 * width * ff,
            transcendentals=2 * rows * ff,
        ),
    )(rows_all, own[0], own[1], other[0], other[1], own[2], other[2], share)


def scatter_kernel(
    part_ref, out_ref, held, half_in, full_in, half_in2, full_in2, z_in,
    load_sem, send1, recv1, send2, recv2, z_send, z_recv,
):
    here = Place()
    width = held.shape[2]
    group = out_ref.shape[1]
    own = here.block("x", 0, 0)
    z_offsets = range(1, here.n_dp)
    greet([here.device(dx=1), here.device(dx=-1), here.device(dy=1), here.device(dy=-1)]
          + [here.device(dz=j) for j in z_offsets])
    started = []
    order = (2, 1, -1, 0)

    def go(copy):
        copy.start()
        started.append(copy)
        return copy

    def flow(number, axis, other, start, span):
        half = span // 2
        whole = pl.ds(start, span)
        parts = (pl.ds(start, half), pl.ds(start + half, half))
        steps = (1, -1)
        halves, loads = {}, {}
        for k, s in enumerate(order):
            block = here.block(axis, 2, s)
            for side in (0, 1):
                halves[k, side] = go(remote(
                    part_ref.at[block, :, parts[side]], half_in.at[number, side, k],
                    send1.at[number, 0, side, k], recv1.at[number, 0, side, k],
                    here.toward(axis, steps[side])))
        for a, first in enumerate((1, -1, 0)):
            for k, s in enumerate(order):
                block = here.block(axis, first, s)
                copy = pltpu.make_async_copy(
                    part_ref.at[block, :, whole], held.at[block, :, whole],
                    load_sem.at[number, a, k])
                copy.start()
                loads[a, k] = copy
        yield
        fulls = {}
        for k, s in enumerate(order):
            for side in (0, 1):
                block = here.block(axis, steps[side], s)
                loads[side, k].wait()
                halves[k, side].wait_recv()
                cols = parts[side]
                summed = held[block, :, cols].astype(F32) + half_in[number, side, k].astype(F32)
                held[block, :, cols] = summed.astype(BF16)
                fulls[k, side] = go(remote(
                    held.at[block, :, whole], full_in.at[number, side, k],
                    send1.at[number, 1, side, k], recv1.at[number, 1, side, k],
                    here.toward(axis, steps[side])))
            yield

        def settle(k):
            block = here.block(axis, 0, order[k])
            loads[2, k].wait()
            fulls[k, 0].wait_recv()
            fulls[k, 1].wait_recv()
            summed = held[block, :, whole].astype(F32) + full_in[number, 0, k].astype(F32)
            summed += full_in[number, 1, k].astype(F32)
            held[block, :, whole] = summed.astype(BF16)
            return block

        block = settle(0)
        last = []
        for side in (0, 1):
            last.append(go(remote(
                held.at[block, :, parts[side]], half_in2.at[number, side],
                send2.at[number, 0, side], recv2.at[number, 0, side],
                here.toward(other, steps[side]))))
        yield
        blocks = [settle(1), settle(2)]
        yield
        settle(3)
        yield
        finals = []
        for side in (0, 1):
            block, cols = blocks[side], parts[side]
            last[side].wait_recv()
            summed = held[block, :, cols].astype(F32) + half_in2[number, side].astype(F32)
            held[block, :, cols] = summed.astype(BF16)
            finals.append(go(remote(
                held.at[block, :, whole], full_in2.at[number, side],
                send2.at[number, 1, side], recv2.at[number, 1, side],
                here.toward(other, steps[side]))))
        yield
        finals[0].wait_recv()
        finals[1].wait_recv()
        summed = held[own, :, whole].astype(F32) + full_in2[number, 0].astype(F32)
        summed += full_in2[number, 1].astype(F32)
        held[own, :, whole] = summed.astype(BF16)
        yield

    take_turns([
        flow(0, "x", "y", 0, width // 2),
        flow(1, "y", "x", width // 2, width // 2),
    ])

    def group_of(z):
        return pl.ds(pl.multiple_of(z * group, group), group)

    last = []
    for j in z_offsets:
        target = lax.rem(here.z + j, here.n_dp)
        last.append(go(remote(
            held.at[own, :, group_of(target)], z_in.at[j - 1],
            z_send.at[j - 1], z_recv.at[j - 1], here.device(dz=j))))
    total = held[own, :, group_of(here.z)].astype(F32)
    for j, copy in zip(z_offsets, last):
        copy.wait_recv()
        total += z_in[j - 1].astype(F32)
    out_ref[...] = total.astype(BF16)
    for copy in started:
        copy.wait_send()


def scatter_all(parts, n_dp):
    blocks, rows, width = parts.shape
    half, quarter, group = width // 2, width // 4, width // n_dp
    dma, vmem = pltpu.SemaphoreType.DMA, pltpu.VMEM
    return pl.pallas_call(
        scatter_kernel,
        out_shape=jax.ShapeDtypeStruct((rows, group), BF16),
        in_specs=[pl.BlockSpec(memory_space=pl.ANY)],
        out_specs=pl.BlockSpec(memory_space=pltpu.VMEM),
        scratch_shapes=[
            vmem((blocks, rows, width), BF16),
            vmem((2, 2, SIDE, rows, quarter), BF16),
            vmem((2, 2, SIDE, rows, half), BF16),
            vmem((2, 2, rows, quarter), BF16),
            vmem((2, 2, rows, half), BF16),
            vmem((n_dp - 1, rows, group), BF16),
            dma((2, 3, SIDE)),
            dma((2, 2, 2, SIDE)), dma((2, 2, 2, SIDE)),
            dma((2, 2, 2)), dma((2, 2, 2)),
            dma((n_dp - 1,)), dma((n_dp - 1,)),
        ],
        compiler_params=pltpu.CompilerParams(
            collective_id=1, has_side_effects=True, vmem_limit_bytes=60 * 2**20
        ),
    )(parts)


def shards(tokens, routes, route_weight, w_gate, w_up, w_down, prev_inputs):
    tok_dev, top = routes.shape
    width = tokens.shape[1]
    n_expert = lax.axis_size("expert")
    n_dp = lax.axis_size("dp")
    col_width = width // n_dp
    counts = route_weight.astype(F32)
    shares = 2.5 * counts / jnp.sum(counts, axis=1, keepdims=True)
    named = jnp.arange(n_expert, dtype=jnp.int32)[:, None, None] == routes[None]
    by_expert = jnp.sum(jnp.where(named, shares[None], 0.0), axis=2)
    by_chip = jnp.broadcast_to(by_expert.reshape(CHIPS, 1, 2 * tok_dev), (CHIPS, 8, 2 * tok_dev))
    whole, arrived, *other = gather_all(tokens, by_chip, w_gate[0], w_up[0], w_down[0])

    history = prev_inputs.reshape(prev_inputs.shape[2], width)
    head = min(HESS_COLS, col_width)
    pieces = jnp.moveaxis(history.reshape(-1, n_dp, col_width), 1, 0)
    heads = jnp.broadcast_to(history[None, :, :head], (n_dp, history.shape[0], head))
    pieces = jnp.concatenate([pieces, heads], axis=2)
    pieces, whole = lax.optimization_barrier((pieces, whole))
    moved = lax.all_to_all(pieces, "dp", split_axis=0, concat_axis=0, tiled=True)

    pairs = arrived[:, 0, :].reshape(CHIPS, 2, tok_dev)
    core = lax.rem(lax.axis_index("expert"), 2)
    pairs = jnp.where(core == 0, pairs, pairs[:, ::-1])
    share = jnp.moveaxis(pairs, 1, 2).reshape(CHIPS * tok_dev, 2)
    out = experts(whole.reshape(CHIPS * tok_dev, width), (w_gate[0], w_up[0], w_down[0]), other, share)
    out, moved = lax.optimization_barrier((out, moved))
    mixed = scatter_all(out.reshape(CHIPS, tok_dev, width), n_dp)

    stacked = moved.reshape(-1, col_width + head)
    hessian = jnp.einsum(
        "rd,rh->dh", stacked[:, :col_width], stacked[:, col_width:], preferred_element_type=F32
    )
    hessian = (hessian * (2.0 / stacked.shape[0]))[:, None, :]
    return (mixed, hessian)


def solution(mesh):
    placed = (
        P("expert", None),
        P("expert", None),
        P("expert", None),
        P("expert", None, "dp"),
        P("expert", None, "dp"),
        P("expert", "dp", None),
        P("dp", "expert", None, None),
    )
    return jax.shard_map(
        shards,
        mesh=mesh,
        in_specs=placed,
        out_specs=(P("expert", "dp"), P("dp", "expert", None)),
        check_vma=False,
    )
```

time: 590 us -> 251 us (0.43)
  waiting for transfers between devices: 463 us -> 0.01 us
  Pallas kernels: 48.9 us -> 235 us
  blocking collectives: 39.6 us -> 0 us
  between operations: 14.2 us -> 0.7 us
    reduce_scatter x4 -> x0, waiting for transfers between devices: 253 us -> none  [the longest x2 204 us: shards(): own = lax.psum_scatter(out, 'expert', scatter_dimension=0, tiled=True)]
    all_gather x2 -> x0, waiting for transfers between devices: 209 us -> none  [shards(): whole = lax.all_gather(block, BOTH, axis=0, tiled=False)]
    pallas_call x2 -> x3, Pallas kernels: 48.9 us -> 235 us  [the longest x1 98.8 us: scatter_all(): pl.pallas_call(scatter_kernel, out_shape=jax.ShapeDtypeStruct((rows, grou...]
    all_gather x1 -> x0, blocking collectives: 26.1 us -> none  [shards(): head = lax.all_gather(history[:, :HESS_COLS], 'dp', axis=0, tiled=True)]
    all_to_all x1 -> x0, blocking collectives: 13.5 us -> none  [shards(): lax.all_to_all(by_expert, 'expert', split_axis=0, concat_axis=0, tiled=True)]
  transfers between devices with their start and end apart: 7 -> 1, of which waited for: 6 -> 0; matrix products, arithmetic and copies ran while one was open for 2% -> 1% of each run, Pallas kernels for 8% -> 22%
where the time goes in v2:
time: 251 us
  Pallas kernels  235 us (94%)
  local copies, waits for them, and re-layouts  7.25 us (3%)
  starting transfers between devices  3.61 us (1%)
  other arithmetic  3.14 us (1%)
    pallas_call x1, Pallas kernels, scatter_all(): pl.pallas_call(scatter_kernel, out_shape=jax.ShapeDtypeStruct((rows, grou...  98.8 us
    pallas_call x1, Pallas kernels, gather_all(): pl.pallas_call(gather_kernel, out_shape=[jax.ShapeDtypeStruct((CHIPS, row...  81.8 us
    pallas_call x1, Pallas kernels, experts(): pl.pallas_call(functools.partial(experts_kernel, steps), grid=(2 * steps,...  54.3 us
  transfers between devices with their start and end apart: 1, of which 0 were waited for; matrix products, arithmetic and copies ran while one was open for 1% of the time, Pallas kernels for 22%

profile of v2, /device:TPU:8, one launch (start us, length us, event | category | flops | bytes accessed | tf_op | source)
XLA Modules:
  0.0 250.8 jit_solution(15841426719305251113)
XLA Ops:
  0.6 0.7 convert_reduce_fusion
  1.3 0.7 multiply_divide_fusion
  2.0 0.7 select_reduce_fusion
  2.8 0.1 broadcast_in_dim.35
  2.8 0.7 slice.16
  3.6 1.3 copy.35
  4.9 0.1 pad_maximum_fusion
  5.1 0.6 broadcast_in_dim.36.share_ref
  5.7 81.8 %shard_map.86 = (bf16[16,64,7168]{2,1,0:T(8,128)(2,1)}, f32[16,8,128]{2,1,0:T(8,128)}, bf16[7168,256]{1,0:T(8,128)(2,1)}, bf16[7168,256]{1,0:T(8,128)(2,1)}, bf16[256,7168]{1,0:T(8,128)(2,1)}) custom-call(bf16[64,7168]{1,0:T(8,128)(2,1)} %tok_ref.1, f32[16,8,128]{2,1,0:T(8,128)} %broadcast_in_dim.36.share_ref, bf16[7168,256]{1,0:T(8,128)(2,1)} %bitcast.21, ...), custom_call_target="tpu_custom_call" | custom-call | tf_op jit(solution)/shard_map/pallas_call | solution.py:227
  87.5 1.5 copy.33
  89.0 3.6 %all-to-all-start = ((bf16[8,64,1024]{2,1,0:T(8,128)(2,1)}), bf16[8,64,1024]{2,1,0:T(8,128)(2,1)S(1)}, u32[]{:S(2)}, u32[]{:S(2)}) async-start(bf16[8,64,1024]{2,1,0:T(8,128)(2,1)} %copy.33), calls=%async_computation | async-start | bytes 2097152 | tf_op jit(solution)/shard_map/all_to_all | solution.py:475
  92.6 0.9 slice_reduce_fusion
  93.5 0.1 reshape_squeeze.3
  93.6 0.2 copy.32
  93.8 0.2 rev.3
  94.0 0.9 broadcast_select_fusion
  94.9 54.3 %shard_map.87 = bf16[1024,7168]{1,0:T(8,128)(2,1)} custom-call(bf16[1024,7168]{1,0:T(8,128)(2,1)} %bitcast.31, bf16[7168,256]{1,0:T(8,128)(2,1)} %bitcast.22, bf16[7168,256]{1,0:T(8,128)(2,1)} %bitcast.24, bf16[7168,256]{1,0:T(8,128)(2,1)} %get-tuple-element.13.gb_ref, bf16[7168,256]{1,0:T(8,128)(2,1)} %get-tuple-element.14.ub_ref, ...), custom_call_target="tpu_custom_call" | custom-call | flops 22548578304 | bytes 51380224 | tf_op jit(solution)/shard_map/pallas_call | solution.py:288
  149.2 0.0 all-to-all-done
  149.2 98.8 %shard_map.88 = bf16[64,896]{1,0:T(8,128)(2,1)} custom-call(bf16[16,64,7168]{2,1,0:T(8,128)(2,1)} %bitcast.19), custom_call_target="tpu_custom_call" | custom-call | tf_op jit(solution)/shard_map/pallas_call | solution.py:433
  248.0 1.2 convolution_multiply_fusion
  249.2 1.6 copy.37
  (1 shorter events, 0.0 us)
Async XLA Ops:
  89.0 60.2 %all-to-all-start = ((bf16[8,64,1024]{2,1,0:T(8,128)(2,1)}), bf16[8,64,1024]{2,1,0:T(8,128)(2,1)S(1)}, u32[]{:S(2)}, u32[]{:S(2)}) async-start(bf16[8,64,1024]{2,1,0:T(8,128)(2,1)} %copy.33), calls=%async_computation | async-start | bytes 2097152 | tf_op jit(solution)/shard_map/all_to_all | solution.py:475

commit v3 on v2

--- a/solution.py
+++ b/solution.py
@@ -12,6 +12,7 @@
 CHIPS = SIDE * SIDE
 UNITS = 56
 SWAP_UNITS = 18
+PARTS = 2
 MESH = pl.DeviceIdType.MESH
 BF16 = jnp.bfloat16
 F32 = jnp.float32
@@ -80,7 +81,7 @@
     flow_send, flow_recv, z_send, z_recv, s_send, s_recv, w_send, w_recv, local_sem,
 ):
     here = Place()
-    width = tok_ref.shape[1]
+    rows, width = tok_ref.shape
     unit = width // UNITS
     offsets = [(i, j) for i in range(SIDE) for j in range(SIDE) if (i, j) != (0, 0)]
     z_steps = (1, -1)
@@ -101,13 +102,14 @@
 
     def flow(number, axis, other, start, span, swapped):
         half = span // 2
+        band = pl.ds((number // 2) * (rows // PARTS), rows // PARTS)
         whole = pl.ds(start, span)
         part_a, part_b = pl.ds(start, half), pl.ds(pl.multiple_of(start + half, unit), half)
 
         def send(t, rel, cols, along, step, local=False):
             block = here.block(axis, *rel)
-            src = tok_ref.at[:, cols] if local else all_ref.at[block, :, cols]
-            return go(remote(src, all_ref.at[block, :, cols], flow_send.at[number, t],
+            src = tok_ref.at[band, cols] if local else all_ref.at[block, band, cols]
+            return go(remote(src, all_ref.at[block, band, cols], flow_send.at[number, t],
                              flow_recv.at[number, t], here.toward(along, step)))
 
         def across(rel, which):
@@ -117,8 +119,9 @@
             slot = (rel[0] % SIDE) * SIDE + rel[1] % SIDE
             for side in which:
                 cols = (part_a, part_b)[side]
-                ref = all_ref.at[block, :, cols]
-                go(remote(ref, ref, z_send.at[side, slot], z_recv.at[side, slot],
+                ref = all_ref.at[block, band, cols]
+                part = number // 2
+                go(remote(ref, ref, z_send.at[part, side, slot], z_recv.at[part, side, slot],
                           here.device(dz=z_steps[side])))
 
         c = {}
@@ -192,29 +195,32 @@
         for n, (i, j) in enumerate(offsets):
             gifts.append(go(remote(share_ref.at[here.block("x", i, j)], shares_ref.at[own],
                                    s_send.at[n], s_recv.at[n], here.device(dx=i, dy=j))))
+        shares_ref[own] = share_ref[own]
         for n, (src, dst) in enumerate(((wg_ref, wg2_ref), (wu_ref, wu2_ref), (wd_ref, wd2_ref))):
             gifts.append(go(remote(src, dst, w_send.at[n], w_recv.at[n], here.partner())))
-        shares_ref[own] = share_ref[own]
-        for _ in range(6):
+            yield
+        for _ in range(4):
             yield
         for gift in gifts:
             gift.wait_recv()
         mine.wait()
 
     fixed = 2 * swap
-    take_turns([
-        flow(0, "x", "y", fixed, width - fixed, False),
-        flow(1, "y", "x", swap_from, swap, True),
-        extras(),
-    ])
+    flows = []
+    for part in range(PARTS):
+        flows.append(flow(2 * part, "x", "y", fixed, width - fixed, False))
+        flows.append(flow(2 * part + 1, "y", "x", swap_from, swap, True))
+    take_turns(flows + [extras()])
     half = swap // 2
-    for side in (0, 1):
-        cols = pl.ds(pl.multiple_of(wanted_from + side * half, unit), half)
-        for i, j in offsets:
-            ref = all_ref.at[here.block("y", i, j), :, cols]
-            slot = i * SIDE + j
-            remote(ref, ref, z_send.at[side, slot], z_recv.at[side, slot],
-                   here.device(dz=z_steps[side])).wait_recv()
+    for part in range(PARTS):
+        band = pl.ds(part * (rows // PARTS), rows // PARTS)
+        for side in (0, 1):
+            cols = pl.ds(pl.multiple_of(wanted_from + side * half, unit), half)
+            for i, j in offsets:
+                ref = all_ref.at[here.block("y", i, j), band, cols]
+                slot = i * SIDE + j
+                remote(ref, ref, z_send.at[part, side, slot], z_recv.at[part, side, slot],
+                       here.device(dz=z_steps[side])).wait_recv()
     for copy in started:
         copy.wait_send()
 
@@ -233,7 +239,8 @@
         in_specs=[vmem, vmem, hbm, hbm, hbm],
         out_specs=[hbm, vmem, hbm, hbm, hbm],
         scratch_shapes=[
-            dma((2, 20)), dma((2, 20)), dma((2, CHIPS)), dma((2, CHIPS)),
+            dma((2 * PARTS, 20)), dma((2 * PARTS, 20)),
+            dma((PARTS, 2, CHIPS)), dma((PARTS, 2, CHIPS)),
             dma((CHIPS - 1,)), dma((CHIPS - 1,)), dma((3,)), dma((3,)), dma(()),
         ],
         compiler_params=pltpu.CompilerParams(
@@ -247,39 +254,39 @@
     sums, hidden,
 ):
     step = pl.program_id(0)
+    ff = ga_ref.shape[1]
 
     @pl.when(step < steps)
     def _():
-        rows = t_ref[...]
-        for n, w_ref in enumerate((ga_ref, ua_ref, gb_ref, ub_ref)):
-            more = jnp.dot(rows, w_ref[...], preferred_element_type=F32)
-
-            @pl.when(step == 0)
-            def _():
-                sums[n] = more
-
-            @pl.when(step > 0)
-            def _():
-                sums[n] += more
+        w = jnp.concatenate([ga_ref[...], ua_ref[...], gb_ref[...], ub_ref[...]], axis=1)
+        more = jnp.dot(t_ref[...], w, preferred_element_type=F32)
+
+        @pl.when(step == 0)
+        def _():
+            sums[...] = more
+
+        @pl.when(step > 0)
+        def _():
+            sums[...] += more
 
     @pl.when(step == steps - 1)
     def _():
         for n in range(2):
-            gate = sums[2 * n]
-            value = gate / (1.0 + jnp.exp(-gate)) * sums[2 * n + 1]
-            hidden[n] = (value * share_ref[:, n : n + 1]).astype(BF16)
+            gate = sums[:, 2 * n * ff : (2 * n + 1) * ff]
+            up = sums[:, (2 * n + 1) * ff : (2 * n + 2) * ff]
+            value = gate / (1.0 + jnp.exp(-gate)) * up
+            hidden[:, n * ff : (n + 1) * ff] = (value * share_ref[:, n : n + 1]).astype(BF16)
 
     @pl.when(step >= steps)
     def _():
-        total = jnp.dot(hidden[0], da_ref[...], preferred_element_type=F32)
-        total += jnp.dot(hidden[1], db_ref[...], preferred_element_type=F32)
-        out_ref[...] = total.astype(BF16)
+        w = jnp.concatenate([da_ref[...], db_ref[...]], axis=0)
+        out_ref[...] = jnp.dot(hidden[...], w, preferred_element_type=F32).astype(BF16)
 
 
 def experts(rows_all, own, other, share):
     rows, width = rows_all.shape
     ff = own[0].shape[1]
-    steps = max(1, width // 1024)
+    steps = max(1, width // 1792)
     cols = width // steps
     first = lambda i: jnp.minimum(i, steps - 1)
     second = lambda i: jnp.maximum(i - steps, 0)
@@ -295,9 +302,9 @@
             pl.BlockSpec((rows, 2), lambda i: (0, 0)),
         ],
         out_specs=pl.BlockSpec((rows, cols), lambda i: (0, second(i))),
-        scratch_shapes=[pltpu.VMEM((4, rows, ff), F32), pltpu.VMEM((2, rows, ff), BF16)],
+        scratch_shapes=[pltpu.VMEM((rows, 4 * ff), F32), pltpu.VMEM((rows, 2 * ff), BF16)],
         compiler_params=pltpu.CompilerParams(
-            dimension_semantics=("arbitrary",), vmem_limit_bytes=56 * 2**20
+            dimension_semantics=("arbitrary",), vmem_limit_bytes=58 * 2**20
         ),
         cost_estimate=pl.CostEstimate(
             flops=12 * rows * width * ff,
@@ -312,7 +319,7 @@
     load_sem, send1, recv1, send2, recv2, z_send, z_recv,
 ):
     here = Place()
-    width = held.shape[2]
+    rows, width = held.shape[1:]
     group = out_ref.shape[1]
     own = here.block("x", 0, 0)
     z_offsets = range(1, here.n_dp)
@@ -328,6 +335,7 @@
 
     def flow(number, axis, other, start, span):
         half = span // 2
+        band = pl.ds((number // 2) * (rows // PARTS), rows // PARTS)
         whole = pl.ds(start, span)
         parts = (pl.ds(start, half), pl.ds(start + half, half))
         steps = (1, -1)
@@ -336,14 +344,14 @@
             block = here.block(axis, 2, s)
             for side in (0, 1):
                 halves[k, side] = go(remote(
-                    part_ref.at[block, :, parts[side]], half_in.at[number, side, k],
+                    part_ref.at[block, band, parts[side]], half_in.at[number, side, k],
                     send1.at[number, 0, side, k], recv1.at[number, 0, side, k],
                     here.toward(axis, steps[side])))
         for a, first in enumerate((1, -1, 0)):
             for k, s in enumerate(order):
                 block = here.block(axis, first, s)
                 copy = pltpu.make_async_copy(
-                    part_ref.at[block, :, whole], held.at[block, :, whole],
+                    part_ref.at[block, band, whole], held.at[block, band, whole],
                     load_sem.at[number, a, k])
                 copy.start()
                 loads[a, k] = copy
@@ -355,10 +363,10 @@
                 loads[side, k].wait()
                 halves[k, side].wait_recv()
                 cols = parts[side]
-                summed = held[block, :, cols].astype(F32) + half_in[number, side, k].astype(F32)
-                held[block, :, cols] = summed.astype(BF16)
+                summed = held[block, band, cols].astype(F32) + half_in[number, side, k].astype(F32)
+                held[block, band, cols] = summed.astype(BF16)
                 fulls[k, side] = go(remote(
-                    held.at[block, :, whole], full_in.at[number, side, k],
+                    held.at[block, band, whole], full_in.at[number, side, k],
                     send1.at[number, 1, side, k], recv1.at[number, 1, side, k],
                     here.toward(axis, steps[side])))
             yield
@@ -368,16 +376,16 @@
             loads[2, k].wait()
             fulls[k, 0].wait_recv()
             fulls[k, 1].wait_recv()
-            summed = held[block, :, whole].astype(F32) + full_in[number, 0, k].astype(F32)
+            summed = held[block, band, whole].astype(F32) + full_in[number, 0, k].astype(F32)
             summed += full_in[number, 1, k].astype(F32)
-            held[block, :, whole] = summed.astype(BF16)
+            held[block, band, whole] = summed.astype(BF16)
             return block
 
         block = settle(0)
         last = []
         for side in (0, 1):
             last.append(go(remote(
-                held.at[block, :, parts[side]], half_in2.at[number, side],
+                held.at[block, band, parts[side]], half_in2.at[number, side],
                 send2.at[number, 0, side], recv2.at[number, 0, side],
                 here.toward(other, steps[side]))))
         yield
@@ -389,46 +397,67 @@
         for side in (0, 1):
             block, cols = blocks[side], parts[side]
             last[side].wait_recv()
-            summed = held[block, :, cols].astype(F32) + half_in2[number, side].astype(F32)
-            held[block, :, cols] = summed.astype(BF16)
+            summed = held[block, band, cols].astype(F32) + half_in2[number, side].astype(F32)
+            held[block, band, cols] = summed.astype(BF16)
             finals.append(go(remote(
-                held.at[block, :, whole], full_in2.at[number, side],
+                held.at[block, band, whole], full_in2.at[number, side],
                 send2.at[number, 1, side], recv2.at[number, 1, side],
                 here.toward(other, steps[side]))))
         yield
         finals[0].wait_recv()
         finals[1].wait_recv()
-        summed = held[own, :, whole].astype(F32) + full_in2[number, 0].astype(F32)
+        summed = held[own, band, whole].astype(F32) + full_in2[number, 0].astype(F32)
         summed += full_in2[number, 1].astype(F32)
-        held[own, :, whole] = summed.astype(BF16)
-        yield
-
-    take_turns([
-        flow(0, "x", "y", 0, width // 2),
-        flow(1, "y", "x", width // 2, width // 2),
-    ])
+        held[own, band, whole] = summed.astype(BF16)
+        yield
+
+    flows = []
+    for part in range(PARTS):
+        flows.append(flow(2 * part, "x", "y", 0, width // 2))
+        flows.append(flow(2 * part + 1, "y", "x", width // 2, width // 2))
 
     def group_of(z):
         return pl.ds(pl.multiple_of(z * group, group), group)
 
-    last = []
-    for j in z_offsets:
-        target = lax.rem(here.z + j, here.n_dp)
-        last.append(go(remote(
-            held.at[own, :, group_of(target)], z_in.at[j - 1],
-            z_send.at[j - 1], z_recv.at[j - 1], here.device(dz=j))))
-    total = held[own, :, group_of(here.z)].astype(F32)
-    for j, copy in zip(z_offsets, last):
-        copy.wait_recv()
-        total += z_in[j - 1].astype(F32)
-    out_ref[...] = total.astype(BF16)
+    def spread(part):
+        band = pl.ds(part * (rows // PARTS), rows // PARTS)
+        copies = []
+        for j in z_offsets:
+            target = lax.rem(here.z + j, here.n_dp)
+            copies.append(go(remote(
+                held.at[own, band, group_of(target)], z_in.at[j - 1, band],
+                z_send.at[part, j - 1], z_recv.at[part, j - 1], here.device(dz=j))))
+        return copies
+
+    def advance(part, count):
+        for _ in range(count):
+            for n in (2 * part, 2 * part + 1):
+                next(flows[n])
+
+    advance(0, 5)
+    advance(1, 1)
+    advance(0, 3)
+    advance(1, 2)
+    advance(0, 1)
+    advance(1, 2)
+    advance(0, 1)
+    last = [spread(0)]
+    advance(1, 5)
+    last.append(spread(1))
+    for part in range(PARTS):
+        band = pl.ds(part * (rows // PARTS), rows // PARTS)
+        total = held[own, band, group_of(here.z)].astype(F32)
+        for j, copy in zip(z_offsets, last[part]):
+            copy.wait_recv()
+            total += z_in[j - 1, band].astype(F32)
+        out_ref[band] = total.astype(BF16)
     for copy in started:
         copy.wait_send()
 
 
 def scatter_all(parts, n_dp):
     blocks, rows, width = parts.shape
-    half, quarter, group = width // 2, width // 4, width // n_dp
+    half, quarter, group, band = width // 2, width // 4, width // n_dp, rows // PARTS
     dma, vmem = pltpu.SemaphoreType.DMA, pltpu.VMEM
     return pl.pallas_call(
         scatter_kernel,
@@ -437,15 +466,15 @@
         out_specs=pl.BlockSpec(memory_space=pltpu.VMEM),
         scratch_shapes=[
             vmem((blocks, rows, width), BF16),
-            vmem((2, 2, SIDE, rows, quarter), BF16),
-            vmem((2, 2, SIDE, rows, half), BF16),
-            vmem((2, 2, rows, quarter), BF16),
-            vmem((2, 2, rows, half), BF16),
+            vmem((2 * PARTS, 2, SIDE, band, quarter), BF16),
+            vmem((2 * PARTS, 2, SIDE, band, half), BF16),
+            vmem((2 * PARTS, 2, band, quarter), BF16),
+            vmem((2 * PARTS, 2, band, half), BF16),
             vmem((n_dp - 1, rows, group), BF16),
-            dma((2, 3, SIDE)),
-            dma((2, 2, 2, SIDE)), dma((2, 2, 2, SIDE)),
-            dma((2, 2, 2)), dma((2, 2, 2)),
-            dma((n_dp - 1,)), dma((n_dp - 1,)),
+            dma((2 * PARTS, 3, SIDE)),
+            dma((2 * PARTS, 2, 2, SIDE)), dma((2 * PARTS, 2, 2, SIDE)),
+            dma((2 * PARTS, 2, 2)), dma((2 * PARTS, 2, 2)),
+            dma((PARTS, n_dp - 1)), dma((PARTS, n_dp - 1)),
         ],
         compiler_params=pltpu.CompilerParams(
             collective_id=1, has_side_effects=True, vmem_limit_bytes=60 * 2**20

time: 251 us -> 225 us (0.90)
  Pallas kernels: 235 us -> 208 us
    pallas_call x1, Pallas kernels: 54.3 us -> 34.5 us  [experts(): pl.pallas_call(functools.partial(experts_kernel, steps), grid=(2 * steps,...]
    pallas_call x1, Pallas kernels: 98.8 us -> 91.8 us  [scatter_all(): pl.pallas_call(scatter_kernel, out_shape=jax.ShapeDtypeStruct((rows, grou...]
  transfers between devices with their start and end apart: 1 -> 1, of which waited for: 0 -> 0; matrix products, arithmetic and copies ran while one was open for 1% -> 1% of each run, Pallas kernels for 22% -> 15%
where the time goes in v3:
time: 225 us; the launch traced here: 224 us
  Pallas kernels  208 us (92%)
  local copies, waits for them, and re-layouts  7.25 us (3%)
  starting transfers between devices  3.74 us (2%)
  other arithmetic  3.14 us (1%)
    pallas_call x1, Pallas kernels, scatter_all(): pl.pallas_call(scatter_kernel, out_shape=jax.ShapeDtypeStruct((rows, grou...  91.8 us
    pallas_call x1, Pallas kernels, gather_all(): pl.pallas_call(gather_kernel, out_shape=[jax.ShapeDtypeStruct((CHIPS, row...  81.6 us
    pallas_call x1, Pallas kernels, experts(): pl.pallas_call(functools.partial(experts_kernel, steps), grid=(2 * steps,...  34.5 us
  transfers between devices with their start and end apart: 1, of which 0 were waited for; matrix products, arithmetic and copies ran while one was open for 1% of the time, Pallas kernels for 15%

profile of v3, /device:TPU:8, one launch (start us, length us, event | category | flops | bytes accessed | tf_op | source)
XLA Modules:
  0.0 223.9 jit_solution(4687667560998347627)
XLA Ops:
  0.6 0.7 convert_reduce_fusion
  1.3 0.7 multiply_divide_fusion
  2.0 0.7 select_reduce_fusion
  2.8 0.1 broadcast_in_dim.35
  2.8 0.7 slice.16
  3.6 1.3 copy.35
  4.9 0.1 pad_maximum_fusion
  5.1 0.6 broadcast_in_dim.36.share_ref
  5.7 81.6 %shard_map.86 = (bf16[16,64,7168]{2,1,0:T(8,128)(2,1)}, f32[16,8,128]{2,1,0:T(8,128)}, bf16[7168,256]{1,0:T(8,128)(2,1)}, bf16[7168,256]{1,0:T(8,128)(2,1)}, bf16[256,7168]{1,0:T(8,128)(2,1)}) custom-call(bf16[64,7168]{1,0:T(8,128)(2,1)} %tok_ref.1, f32[16,8,128]{2,1,0:T(8,128)} %broadcast_in_dim.36.share_ref, bf16[7168,256]{1,0:T(8,128)(2,1)} %bitcast.21, ...), custom_call_target="tpu_custom_call" | custom-call | tf_op jit(solution)/shard_map/pallas_call | solution.py:233
  87.3 1.5 copy.33
  88.8 3.7 %all-to-all-start = ((bf16[8,64,1024]{2,1,0:T(8,128)(2,1)}), bf16[8,64,1024]{2,1,0:T(8,128)(2,1)S(1)}, u32[]{:S(2)}, u32[]{:S(2)}) async-start(bf16[8,64,1024]{2,1,0:T(8,128)(2,1)} %copy.33), calls=%async_computation | async-start | bytes 2097152 | tf_op jit(solution)/shard_map/all_to_all | solution.py:504
  92.6 0.9 slice_reduce_fusion
  93.5 0.1 reshape_squeeze.3
  93.5 0.2 copy.32
  93.8 0.2 rev.3
  94.0 0.9 broadcast_select_fusion
  94.9 34.5 %shard_map.87 = bf16[1024,7168]{1,0:T(8,128)(2,1)} custom-call(bf16[1024,7168]{1,0:T(8,128)(2,1)} %bitcast.31, bf16[7168,256]{1,0:T(8,128)(2,1)} %bitcast.22, bf16[7168,256]{1,0:T(8,128)(2,1)} %bitcast.24, bf16[7168,256]{1,0:T(8,128)(2,1)} %get-tuple-element.13.gb_ref, bf16[7168,256]{1,0:T(8,128)(2,1)} %get-tuple-element.14.ub_ref, ...), custom_call_target="tpu_custom_call" | custom-call | flops 22548578304 | bytes 51380224 | tf_op jit(solution)/shard_map/pallas_call | solution.py:295
  129.4 0.0 all-to-all-done
  129.4 91.8 %shard_map.88 = bf16[64,896]{1,0:T(8,128)(2,1)} custom-call(bf16[16,64,7168]{2,1,0:T(8,128)(2,1)} %bitcast.19), custom_call_target="tpu_custom_call" | custom-call | tf_op jit(solution)/shard_map/pallas_call | solution.py:462
  221.2 1.2 convolution_multiply_fusion
  222.4 1.6 copy.37
  (1 shorter events, 0.0 us)
Async XLA Ops:
  88.8 40.5 %all-to-all-start = ((bf16[8,64,1024]{2,1,0:T(8,128)(2,1)}), bf16[8,64,1024]{2,1,0:T(8,128)(2,1)S(1)}, u32[]{:S(2)}, u32[]{:S(2)}) async-start(bf16[8,64,1024]{2,1,0:T(8,128)(2,1)} %copy.33), calls=%async_computation | async-start | bytes 2097152 | tf_op jit(solution)/shard_map/all_to_all | solution.py:504

commit v4 on v3

--- a/solution.py
+++ b/solution.py
@@ -13,6 +13,7 @@
 UNITS = 56
 SWAP_UNITS = 18
 PARTS = 2
+BANDS = ((0, 48), (48, 16))
 MESH = pl.DeviceIdType.MESH
 BF16 = jnp.bfloat16
 F32 = jnp.float32
@@ -127,6 +128,7 @@
         c = {}
         c[0] = send(0, (0, 0), whole, axis, 1, True)
         c[1] = send(1, (0, 0), whole, axis, -1, True)
+        yield
         c[2] = send(2, (0, 0), whole, other, 1, True)
         c[3] = send(3, (0, 0), whole, other, -1, True)
         yield
@@ -315,39 +317,56 @@
 
 
 def scatter_kernel(
-    part_ref, out_ref, held, half_in, full_in, half_in2, full_in2, z_in,
-    load_sem, send1, recv1, send2, recv2, z_send, z_recv,
+    layout, part_ref, out_ref, held, swap_in, total, z_in, load_sem, send1, recv1, send2, recv2,
+    swap_send, swap_recv, z_send, z_recv, *landing,
 ):
     here = Place()
-    rows, width = held.shape[1:]
+    width = held.shape[2]
     group = out_ref.shape[1]
+    unit = width // UNITS
     own = here.block("x", 0, 0)
     z_offsets = range(1, here.n_dp)
     greet([here.device(dx=1), here.device(dx=-1), here.device(dy=1), here.device(dy=-1)]
           + [here.device(dz=j) for j in z_offsets])
     started = []
     order = (2, 1, -1, 0)
+    steps = (1, -1)
+    parity = lax.rem(here.z, 2)
+    given_from, kept_from = parity * (width // 4), (1 - parity) * (width // 4)
+    given_half = width // 8
 
     def go(copy):
         copy.start()
         started.append(copy)
         return copy
 
-    def flow(number, axis, other, start, span):
-        half = span // 2
-        band = pl.ds((number // 2) * (rows // PARTS), rows // PARTS)
-        whole = pl.ds(start, span)
-        parts = (pl.ds(start, half), pl.ds(start + half, half))
-        steps = (1, -1)
+    def columns(start, span):
+        return pl.ds(pl.multiple_of(start, unit), span)
+
+    def swap(part):
+        band = pl.ds(*BANDS[part])
+        copies = {}
+        for a, first in enumerate(order):
+            for k, s in enumerate(order):
+                block = here.block("y", first, s)
+                for side in (0, 1):
+                    cols = columns(given_from + side * given_half, given_half)
+                    copies[a, k, side] = go(remote(
+                        part_ref.at[block, band, cols], swap_in.at[side, 4 * a + k, band],
+                        swap_send.at[part, side, 4 * a + k], swap_recv.at[part, side, 4 * a + k],
+                        here.device(dz=steps[side])))
+        return copies
+
+    def flow(number, part, axis, other, start, spans, swaps):
+        half_in, full_in, half_in2, full_in2 = landing[4 * number : 4 * number + 4]
+        band = pl.ds(*BANDS[part])
+        whole = columns(start, sum(spans))
+        parts = (columns(start, spans[0]), columns(start + spans[0], spans[1]))
+        slots = (pl.ds(0, spans[0]), pl.ds(0, spans[1]))
         halves, loads = {}, {}
-        for k, s in enumerate(order):
-            block = here.block(axis, 2, s)
-            for side in (0, 1):
-                halves[k, side] = go(remote(
-                    part_ref.at[block, band, parts[side]], half_in.at[number, side, k],
-                    send1.at[number, 0, side, k], recv1.at[number, 0, side, k],
-                    here.toward(axis, steps[side])))
-        for a, first in enumerate((1, -1, 0)):
+        for a, first in enumerate(order):
+            if a == 0 and swaps is None:
+                continue
             for k, s in enumerate(order):
                 block = here.block(axis, first, s)
                 copy = pltpu.make_async_copy(
@@ -355,29 +374,53 @@
                     load_sem.at[number, a, k])
                 copy.start()
                 loads[a, k] = copy
+
+        def ready(a, k):
+            loads[a, k].wait()
+            if swaps is None:
+                return
+            block = here.block(axis, order[a], order[k])
+            for side in (0, 1):
+                swaps[a, k, side].wait_recv()
+                both = held[block, band, parts[side]].astype(F32)
+                both += swap_in[side, 4 * a + k, band].astype(F32)
+                held[block, band, parts[side]] = both.astype(BF16)
+
+        for k, s in enumerate(order):
+            block = here.block(axis, 2, s)
+            source = part_ref
+            if swaps is not None:
+                ready(0, k)
+                source = held
+            for side in (0, 1):
+                halves[k, side] = go(remote(
+                    source.at[block, band, parts[side]], half_in.at[side, k, :, slots[side]],
+                    send1.at[number, 0, side, k], recv1.at[number, 0, side, k],
+                    here.toward(axis, steps[side])))
         yield
         fulls = {}
         for k, s in enumerate(order):
             for side in (0, 1):
                 block = here.block(axis, steps[side], s)
-                loads[side, k].wait()
+                ready(1 + side, k)
                 halves[k, side].wait_recv()
                 cols = parts[side]
-                summed = held[block, band, cols].astype(F32) + half_in[number, side, k].astype(F32)
+                summed = held[block, band, cols].astype(F32)
+                summed += half_in[side, k, :, slots[side]].astype(F32)
                 held[block, band, cols] = summed.astype(BF16)
                 fulls[k, side] = go(remote(
-                    held.at[block, band, whole], full_in.at[number, side, k],
+                    held.at[block, band, whole], full_in.at[side, k],
                     send1.at[number, 1, side, k], recv1.at[number, 1, side, k],
                     here.toward(axis, steps[side])))
             yield
 
         def settle(k):
             block = here.block(axis, 0, order[k])
-            loads[2, k].wait()
+            ready(3, k)
             fulls[k, 0].wait_recv()
             fulls[k, 1].wait_recv()
-            summed = held[block, band, whole].astype(F32) + full_in[number, 0, k].astype(F32)
-            summed += full_in[number, 1, k].astype(F32)
+            summed = held[block, band, whole].astype(F32) + full_in[0, k].astype(F32)
+            summed += full_in[1, k].astype(F32)
             held[block, band, whole] = summed.astype(BF16)
             return block
 
@@ -385,7 +428,7 @@
         last = []
         for side in (0, 1):
             last.append(go(remote(
-                held.at[block, band, parts[side]], half_in2.at[number, side],
+                held.at[block, band, parts[side]], half_in2.at[side, :, slots[side]],
                 send2.at[number, 0, side], recv2.at[number, 0, side],
                 here.toward(other, steps[side]))))
         yield
@@ -397,84 +440,143 @@
         for side in (0, 1):
             block, cols = blocks[side], parts[side]
             last[side].wait_recv()
-            summed = held[block, band, cols].astype(F32) + half_in2[number, side].astype(F32)
+            summed = held[block, band, cols].astype(F32)
+            summed += half_in2[side, :, slots[side]].astype(F32)
             held[block, band, cols] = summed.astype(BF16)
             finals.append(go(remote(
-                held.at[block, band, whole], full_in2.at[number, side],
+                held.at[block, band, whole], full_in2.at[side],
                 send2.at[number, 1, side], recv2.at[number, 1, side],
                 here.toward(other, steps[side]))))
         yield
         finals[0].wait_recv()
         finals[1].wait_recv()
-        summed = held[own, band, whole].astype(F32) + full_in2[number, 0].astype(F32)
-        summed += full_in2[number, 1].astype(F32)
+        summed = held[own, band, whole].astype(F32) + full_in2[0].astype(F32)
+        summed += full_in2[1].astype(F32)
         held[own, band, whole] = summed.astype(BF16)
         yield
 
-    flows = []
-    for part in range(PARTS):
-        flows.append(flow(2 * part, "x", "y", 0, width // 2))
-        flows.append(flow(2 * part + 1, "y", "x", width // 2, width // 2))
+    quarter = here.n_dp // 4
+
+    def holds(source, target):
+        odd = lax.rem(source, 2)
+        wanted = jnp.where(target < quarter, 1, 0)
+        return jnp.logical_or(target >= 2 * quarter, odd == wanted)
 
     def group_of(z):
-        return pl.ds(pl.multiple_of(z * group, group), group)
+        return columns(z * group, group)
 
     def spread(part):
-        band = pl.ds(part * (rows // PARTS), rows // PARTS)
+        band = pl.ds(*BANDS[part])
         copies = []
         for j in z_offsets:
             target = lax.rem(here.z + j, here.n_dp)
-            copies.append(go(remote(
+            copy = remote(
                 held.at[own, band, group_of(target)], z_in.at[j - 1, band],
-                z_send.at[part, j - 1], z_recv.at[part, j - 1], here.device(dz=j))))
+                z_send.at[part, j - 1], z_recv.at[part, j - 1], here.device(dz=j))
+            pl.when(holds(here.z, target))(copy.start)
+            copies.append((copy, target))
         return copies
 
-    def advance(part, count):
+    def finish(part, copies):
+        band = pl.ds(*BANDS[part])
+        mine = held[own, band, group_of(here.z)].astype(F32)
+        total[band] = jnp.where(holds(here.z, here.z), mine, 0.0)
+        for j, (copy, target) in zip(z_offsets, copies):
+            source = lax.rem(here.z - j + here.n_dp, here.n_dp)
+
+            @pl.when(holds(source, here.z))
+            def _():
+                copy.wait_recv()
+                total[band] += z_in[j - 1, band].astype(F32)
+
+            pl.when(holds(here.z, target))(copy.wait_send)
+        out_ref[band] = total[band].astype(BF16)
+
+    starts = (5 * width // 8, width // 2, kept_from)
+    flows, swaps = {}, {}
+    axes = (("x", "y"), ("y", "x"), ("y", "x"))
+
+    def begin(name, part):
+        n = "abc".index(name)
+        flows[name, part] = flow(3 * part + n, part, *axes[n], starts[n], layout[n],
+                                 swaps[part] if n == 2 else None)
+
+    def advance(names, part, count):
         for _ in range(count):
-            for n in (2 * part, 2 * part + 1):
-                next(flows[n])
-
-    advance(0, 5)
-    advance(1, 1)
-    advance(0, 3)
-    advance(1, 2)
-    advance(0, 1)
-    advance(1, 2)
-    advance(0, 1)
+            for name in names:
+                next(flows[name, part])
+
+    begin("a", 0)
+    begin("b", 0)
+    advance("ab", 0, 1)
+    swaps[0] = swap(0)
+    swaps[1] = swap(1)
+    begin("c", 0)
+    advance("ab", 0, 2)
+    advance("c", 0, 1)
+    advance("ab", 0, 2)
+    advance("c", 0, 2)
+    begin("a", 1)
+    begin("b", 1)
+    advance("ab", 1, 1)
+    advance("c", 0, 2)
+    advance("ab", 0, 3)
+    advance("ab", 1, 2)
+    advance("c", 0, 1)
+    begin("c", 1)
+    advance("c", 1, 1)
+    advance("ab", 1, 2)
+    advance("ab", 0, 1)
+    advance("c", 0, 2)
+    advance("c", 1, 4)
+    advance("ab", 0, 1)
+    advance("c", 0, 1)
+    advance("ab", 1, 3)
+    advance("c", 0, 1)
     last = [spread(0)]
-    advance(1, 5)
+    advance("c", 1, 3)
+    advance("ab", 1, 1)
+    advance("c", 1, 1)
+    advance("ab", 1, 1)
+    advance("c", 1, 1)
     last.append(spread(1))
-    for part in range(PARTS):
-        band = pl.ds(part * (rows // PARTS), rows // PARTS)
-        total = held[own, band, group_of(here.z)].astype(F32)
-        for j, copy in zip(z_offsets, last[part]):
-            copy.wait_recv()
-            total += z_in[j - 1, band].astype(F32)
-        out_ref[band] = total.astype(BF16)
+    for part in range(2):
+        finish(part, last[part])
     for copy in started:
         copy.wait_send()
 
 
 def scatter_all(parts, n_dp):
     blocks, rows, width = parts.shape
-    half, quarter, group, band = width // 2, width // 4, width // n_dp, rows // PARTS
+    unit, group = width // UNITS, width // n_dp
+    layout = ((11 * unit, 10 * unit), (4 * unit, 3 * unit), (7 * unit, 7 * unit))
     dma, vmem = pltpu.SemaphoreType.DMA, pltpu.VMEM
+    landing = []
+    for part in range(2):
+        for first, second in layout:
+            band = BANDS[part][1]
+            landing += [
+                vmem((2, SIDE, band, first), BF16),
+                vmem((2, SIDE, band, first + second), BF16),
+                vmem((2, band, first), BF16),
+                vmem((2, band, first + second), BF16),
+            ]
     return pl.pallas_call(
-        scatter_kernel,
+        functools.partial(scatter_kernel, layout),
         out_shape=jax.ShapeDtypeStruct((rows, group), BF16),
         in_specs=[pl.BlockSpec(memory_space=pl.ANY)],
         out_specs=pl.BlockSpec(memory_space=pltpu.VMEM),
         scratch_shapes=[
             vmem((blocks, rows, width), BF16),
-            vmem((2 * PARTS, 2, SIDE, band, quarter), BF16),
-            vmem((2 * PARTS, 2, SIDE, band, half), BF16),
-            vmem((2 * PARTS, 2, band, quarter), BF16),
-            vmem((2 * PARTS, 2, band, half), BF16),
+            vmem((2, blocks, rows, width // 8), BF16),
+            vmem((rows, group), F32),
             vmem((n_dp - 1, rows, group), BF16),
-            dma((2 * PARTS, 3, SIDE)),
-            dma((2 * PARTS, 2, 2, SIDE)), dma((2 * PARTS, 2, 2, SIDE)),
-            dma((2 * PARTS, 2, 2)), dma((2 * PARTS, 2, 2)),
-            dma((PARTS, n_dp - 1)), dma((PARTS, n_dp - 1)),
+            dma((6, SIDE, SIDE)),
+            dma((6, 2, 2, SIDE)), dma((6, 2, 2, SIDE)),
+            dma((6, 2, 2)), dma((6, 2, 2)),
+            dma((2, 2, blocks)), dma((2, 2, blocks)),
+            dma((2, n_dp - 1)), dma((2, n_dp - 1)),
+            *landing,
         ],
         compiler_params=pltpu.CompilerParams(
             collective_id=1, has_side_effects=True, vmem_limit_bytes=60 * 2**20

time: 225 us -> 215 us (0.956)
  Pallas kernels: 208 us -> 198 us
    pallas_call x1, Pallas kernels: 91.8 us -> 81.8 us  [scatter_all(): pl.pallas_call(functools.partial(scatter_kernel, layout), out_shape=jax.S...]
  transfers between devices with their start and end apart: 1 -> 1, of which waited for: 0 -> 0; matrix products, arithmetic and copies ran while one was open for 1% -> 1% of each run, Pallas kernels for 15% -> 16%
where the time goes in v4:
time: 215 us; the launch traced here: 214 us
  Pallas kernels  198 us (92%)
  local copies, waits for them, and re-layouts  7.25 us (3%)
  starting transfers between devices  3.74 us (2%)
  other arithmetic  3.14 us (1%)
    pallas_call x1, Pallas kernels, gather_all(): pl.pallas_call(gather_kernel, out_shape=[jax.ShapeDtypeStruct((CHIPS, row...  82 us
    pallas_call x1, Pallas kernels, scatter_all(): pl.pallas_call(functools.partial(scatter_kernel, layout), out_shape=jax.S...  81.8 us
    pallas_call x1, Pallas kernels, experts(): pl.pallas_call(functools.partial(experts_kernel, steps), grid=(2 * steps,...  34.5 us
  transfers between devices with their start and end apart: 1, of which 0 were waited for; matrix products, arithmetic and copies ran while one was open for 1% of the time, Pallas kernels for 16%

profile of v4, /device:TPU:8, one launch (start us, length us, event | category | flops | bytes accessed | tf_op | source)
XLA Modules:
  0.0 214.4 jit_solution(16205514725381984741)
XLA Ops:
  0.6 0.7 convert_reduce_fusion
  1.3 0.7 multiply_divide_fusion
  2.0 0.7 select_reduce_fusion
  2.8 0.1 broadcast_in_dim.35
  2.8 0.7 slice.16
  3.6 1.3 copy.35
  4.9 0.1 pad_maximum_fusion
  5.1 0.6 broadcast_in_dim.36.share_ref
  5.7 82.0 %shard_map.86 = (bf16[16,64,7168]{2,1,0:T(8,128)(2,1)}, f32[16,8,128]{2,1,0:T(8,128)}, bf16[7168,256]{1,0:T(8,128)(2,1)}, bf16[7168,256]{1,0:T(8,128)(2,1)}, bf16[256,7168]{1,0:T(8,128)(2,1)}) custom-call(bf16[64,7168]{1,0:T(8,128)(2,1)} %tok_ref.1, f32[16,8,128]{2,1,0:T(8,128)} %broadcast_in_dim.36.share_ref, bf16[7168,256]{1,0:T(8,128)(2,1)} %bitcast.21, ...), custom_call_target="tpu_custom_call" | custom-call | tf_op jit(solution)/shard_map/pallas_call | solution.py:235
  87.7 1.5 copy.33
  89.3 3.7 %all-to-all-start = ((bf16[8,64,1024]{2,1,0:T(8,128)(2,1)}), bf16[8,64,1024]{2,1,0:T(8,128)(2,1)S(1)}, u32[]{:S(2)}, u32[]{:S(2)}) async-start(bf16[8,64,1024]{2,1,0:T(8,128)(2,1)} %copy.33), calls=%async_computation | async-start | bytes 2097152 | tf_op jit(solution)/shard_map/all_to_all | solution.py:606
  93.0 0.9 slice_reduce_fusion
  93.9 0.1 reshape_squeeze.3
  94.0 0.2 copy.32
  94.2 0.2 rev.3
  94.4 0.9 broadcast_select_fusion
  95.3 34.5 %shard_map.87 = bf16[1024,7168]{1,0:T(8,128)(2,1)} custom-call(bf16[1024,7168]{1,0:T(8,128)(2,1)} %bitcast.31, bf16[7168,256]{1,0:T(8,128)(2,1)} %bitcast.22, bf16[7168,256]{1,0:T(8,128)(2,1)} %bitcast.24, bf16[7168,256]{1,0:T(8,128)(2,1)} %get-tuple-element.13.gb_ref, bf16[7168,256]{1,0:T(8,128)(2,1)} %get-tuple-element.14.ub_ref, ...), custom_call_target="tpu_custom_call" | custom-call | flops 22548578304 | bytes 51380224 | tf_op jit(solution)/shard_map/pallas_call | solution.py:297
  129.8 0.0 all-to-all-done
  129.8 81.8 %shard_map.88 = bf16[64,896]{1,0:T(8,128)(2,1)} custom-call(bf16[16,64,7168]{2,1,0:T(8,128)(2,1)} %bitcast.19), custom_call_target="tpu_custom_call" | custom-call | tf_op jit(solution)/shard_map/pallas_call | solution.py:564
  211.6 1.2 convolution_multiply_fusion
  212.8 1.6 copy.37
  (1 shorter events, 0.0 us)
Async XLA Ops:
  89.3 40.5 %all-to-all-start = ((bf16[8,64,1024]{2,1,0:T(8,128)(2,1)}), bf16[8,64,1024]{2,1,0:T(8,128)(2,1)S(1)}, u32[]{:S(2)}, u32[]{:S(2)}) async-start(bf16[8,64,1024]{2,1,0:T(8,128)(2,1)} %copy.33), calls=%async_computation | async-start | bytes 2097152 | tf_op jit(solution)/shard_map/all_to_all | solution.py:606

commit v5 on v4

--- a/solution.py
+++ b/solution.py
@@ -79,7 +79,7 @@
 def gather_kernel(
     tok_ref, share_ref, wg_ref, wu_ref, wd_ref,
     all_ref, shares_ref, wg2_ref, wu2_ref, wd2_ref,
-    flow_send, flow_recv, z_send, z_recv, s_send, s_recv, w_send, w_recv, local_sem,
+    held, flow_send, flow_recv, z_send, z_recv, s_send, s_recv, w_send, w_recv, flush_sem,
 ):
     here = Place()
     rows, width = tok_ref.shape
@@ -109,8 +109,8 @@
 
         def send(t, rel, cols, along, step, local=False):
             block = here.block(axis, *rel)
-            src = tok_ref.at[band, cols] if local else all_ref.at[block, band, cols]
-            return go(remote(src, all_ref.at[block, band, cols], flow_send.at[number, t],
+            src = tok_ref.at[band, cols] if local else held.at[block, band, cols]
+            return go(remote(src, held.at[block, band, cols], flow_send.at[number, t],
                              flow_recv.at[number, t], here.toward(along, step)))
 
         def across(rel, which):
@@ -120,7 +120,7 @@
             slot = (rel[0] % SIDE) * SIDE + rel[1] % SIDE
             for side in which:
                 cols = (part_a, part_b)[side]
-                ref = all_ref.at[block, band, cols]
+                ref = held.at[block, band, cols]
                 part = number // 2
                 go(remote(ref, ref, z_send.at[part, side, slot], z_recv.at[part, side, slot],
                           here.device(dz=z_steps[side])))
@@ -190,9 +190,8 @@
         yield
 
     def extras():
-        mine = pltpu.make_async_copy(tok_ref, all_ref.at[own], local_sem)
-        mine.start()
-        yield
+        yield
+        held[own] = tok_ref[...]
         gifts = []
         for n, (i, j) in enumerate(offsets):
             gifts.append(go(remote(share_ref.at[here.block("x", i, j)], shares_ref.at[own],
@@ -205,7 +204,6 @@
             yield
         for gift in gifts:
             gift.wait_recv()
-        mine.wait()
 
     fixed = 2 * swap
     flows = []
@@ -213,18 +211,32 @@
         flows.append(flow(2 * part, "x", "y", fixed, width - fixed, False))
         flows.append(flow(2 * part + 1, "y", "x", swap_from, swap, True))
     take_turns(flows + [extras()])
+    flushes = []
+
+    def flush(start, span):
+        cols = pl.ds(start, span)
+        copy = pltpu.make_async_copy(
+            held.at[:, :, cols], all_ref.at[:, :, cols], flush_sem.at[len(flushes)])
+        copy.start()
+        flushes.append(copy)
+
+    flush(fixed, width - fixed)
+    flush(swap_from, swap)
     half = swap // 2
     for part in range(PARTS):
         band = pl.ds(part * (rows // PARTS), rows // PARTS)
         for side in (0, 1):
             cols = pl.ds(pl.multiple_of(wanted_from + side * half, unit), half)
             for i, j in offsets:
-                ref = all_ref.at[here.block("y", i, j), band, cols]
+                ref = held.at[here.block("y", i, j), band, cols]
                 slot = i * SIDE + j
                 remote(ref, ref, z_send.at[part, side, slot], z_recv.at[part, side, slot],
                        here.device(dz=z_steps[side])).wait_recv()
+    flush(wanted_from, swap)
     for copy in started:
         copy.wait_send()
+    for copy in flushes:
+        copy.wait()
 
 
 def gather_all(tokens, share, w_gate, w_up, w_down):
@@ -241,9 +253,10 @@
         in_specs=[vmem, vmem, hbm, hbm, hbm],
         out_specs=[hbm, vmem, hbm, hbm, hbm],
         scratch_shapes=[
+            pltpu.VMEM((CHIPS, rows, width), BF16),
             dma((2 * PARTS, 20)), dma((2 * PARTS, 20)),
             dma((PARTS, 2, CHIPS)), dma((PARTS, 2, CHIPS)),
-            dma((CHIPS - 1,)), dma((CHIPS - 1,)), dma((3,)), dma((3,)), dma(()),
+            dma((CHIPS - 1,)), dma((CHIPS - 1,)), dma((3,)), dma((3,)), dma((3,)),
         ],
         compiler_params=pltpu.CompilerParams(
             collective_id=0, has_side_effects=True, vmem_limit_bytes=60 * 2**20
@@ -347,14 +360,13 @@
         band = pl.ds(*BANDS[part])
         copies = {}
         for a, first in enumerate(order):
-            for k, s in enumerate(order):
-                block = here.block("y", first, s)
-                for side in (0, 1):
-                    cols = columns(given_from + side * given_half, given_half)
-                    copies[a, k, side] = go(remote(
-                        part_ref.at[block, band, cols], swap_in.at[side, 4 * a + k, band],
-                        swap_send.at[part, side, 4 * a + k], swap_recv.at[part, side, 4 * a + k],
-                        here.device(dz=steps[side])))
+            line = lax.rem(here.y + first + SIDE, SIDE)
+            for side in (0, 1):
+                cols = columns(given_from + side * given_half, given_half)
+                copies[a, side] = go(remote(
+                    part_ref.at[:, line, band, cols], swap_in.at[side, a, :, band],
+                    swap_send.at[part, side, a], swap_recv.at[part, side, a],
+                    here.device(dz=steps[side])))
         return copies
 
     def flow(number, part, axis, other, start, spans, swaps):
@@ -370,8 +382,8 @@
             for k, s in enumerate(order):
                 block = here.block(axis, first, s)
                 copy = pltpu.make_async_copy(
-                    part_ref.at[block, band, whole], held.at[block, band, whole],
-                    load_sem.at[number, a, k])
+                    part_ref.at[block // SIDE, lax.rem(block, SIDE), band, whole],
+                    held.at[block, band, whole], load_sem.at[number, a, k])
                 copy.start()
                 loads[a, k] = copy
 
@@ -380,21 +392,25 @@
             if swaps is None:
                 return
             block = here.block(axis, order[a], order[k])
+            place = lax.rem(here.x + order[k] + SIDE, SIDE)
             for side in (0, 1):
-                swaps[a, k, side].wait_recv()
+                if k == 0:
+                    swaps[a, side].wait_recv()
                 both = held[block, band, parts[side]].astype(F32)
-                both += swap_in[side, 4 * a + k, band].astype(F32)
+                both += swap_in[side, a, place, band].astype(F32)
                 held[block, band, parts[side]] = both.astype(BF16)
 
         for k, s in enumerate(order):
             block = here.block(axis, 2, s)
-            source = part_ref
             if swaps is not None:
                 ready(0, k)
-                source = held
             for side in (0, 1):
+                source = held.at[block, band, parts[side]]
+                if swaps is None:
+                    source = part_ref.at[
+                        block // SIDE, lax.rem(block, SIDE), band, parts[side]]
                 halves[k, side] = go(remote(
-                    source.at[block, band, parts[side]], half_in.at[side, k, :, slots[side]],
+                    source, half_in.at[side, k, :, slots[side]],
                     send1.at[number, 0, side, k], recv1.at[number, 0, side, k],
                     here.toward(axis, steps[side])))
         yield
@@ -568,20 +584,20 @@
         out_specs=pl.BlockSpec(memory_space=pltpu.VMEM),
         scratch_shapes=[
             vmem((blocks, rows, width), BF16),
-            vmem((2, blocks, rows, width // 8), BF16),
+            vmem((2, SIDE, SIDE, rows, width // 8), BF16),
             vmem((rows, group), F32),
             vmem((n_dp - 1, rows, group), BF16),
             dma((6, SIDE, SIDE)),
             dma((6, 2, 2, SIDE)), dma((6, 2, 2, SIDE)),
             dma((6, 2, 2)), dma((6, 2, 2)),
-            dma((2, 2, blocks)), dma((2, 2, blocks)),
+            dma((2, 2, SIDE)), dma((2, 2, SIDE)),
             dma((2, n_dp - 1)), dma((2, n_dp - 1)),
             *landing,
         ],
         compiler_params=pltpu.CompilerParams(
             collective_id=1, has_side_effects=True, vmem_limit_bytes=60 * 2**20
         ),
-    )(parts)
+    )(parts.reshape(SIDE, SIDE, rows, width))
 
 
 def shards(tokens, routes, route_weight, w_gate, w_up, w_down, prev_inputs):

time: 215 us -> 216 us (level)
  no operation moved by 1% of the time
where the time goes in v5:
time: 216 us; the launch traced here: 215 us
  Pallas kernels  199 us (92%)
  local copies, waits for them, and re-layouts  7.25 us (3%)
  starting transfers between devices  3.74 us (2%)
  other arithmetic  3.14 us (1%)
    pallas_call x1, Pallas kernels, gather_all(): pl.pallas_call(gather_kernel, out_shape=[jax.ShapeDtypeStruct((CHIPS, row...  83.6 us
    pallas_call x1, Pallas kernels, scatter_all(): pl.pallas_call(functools.partial(scatter_kernel, layout), out_shape=jax.S...  80.4 us
    pallas_call x1, Pallas kernels, experts(): pl.pallas_call(functools.partial(experts_kernel, steps), grid=(2 * steps,...  34.5 us
  transfers between devices with their start and end apart: 1, of which 0 were waited for; matrix products, arithmetic and copies ran while one was open for 1% of the time, Pallas kernels for 16%

profile of v5, /device:TPU:8, one launch (start us, length us, event | category | flops | bytes accessed | tf_op | source)
XLA Modules:
  0.0 214.6 jit_solution(14692918553288504868)
XLA Ops:
  0.6 0.7 convert_reduce_fusion
  1.3 0.7 multiply_divide_fusion
  2.0 0.7 select_reduce_fusion
  2.8 0.1 broadcast_in_dim.35
  2.8 0.7 slice.16
  3.6 1.3 copy.35
  4.9 0.1 pad_maximum_fusion
  5.1 0.6 broadcast_in_dim.36.share_ref
  5.7 83.6 %shard_map.86 = (bf16[16,64,7168]{2,1,0:T(8,128)(2,1)}, f32[16,8,128]{2,1,0:T(8,128)}, bf16[7168,256]{1,0:T(8,128)(2,1)}, bf16[7168,256]{1,0:T(8,128)(2,1)}, bf16[256,7168]{1,0:T(8,128)(2,1)}) custom-call(bf16[64,7168]{1,0:T(8,128)(2,1)} %tok_ref.1, f32[16,8,128]{2,1,0:T(8,128)} %broadcast_in_dim.36.share_ref, bf16[7168,256]{1,0:T(8,128)(2,1)} %bitcast.21, ...), custom_call_target="tpu_custom_call" | custom-call | tf_op jit(solution)/shard_map/pallas_call | solution.py:247
  89.3 1.5 copy.33
  90.9 3.7 %all-to-all-start = ((bf16[8,64,1024]{2,1,0:T(8,128)(2,1)}), bf16[8,64,1024]{2,1,0:T(8,128)(2,1)S(1)}, u32[]{:S(2)}, u32[]{:S(2)}) async-start(bf16[8,64,1024]{2,1,0:T(8,128)(2,1)} %copy.33), calls=%async_computation | async-start | bytes 2097152 | tf_op jit(solution)/shard_map/all_to_all | solution.py:622
  94.6 0.9 slice_reduce_fusion
  95.5 0.1 reshape_squeeze.3
  95.6 0.2 copy.32
  95.8 0.2 rev.3
  96.0 0.9 broadcast_select_fusion
  96.9 34.5 %shard_map.87 = bf16[1024,7168]{1,0:T(8,128)(2,1)} custom-call(bf16[1024,7168]{1,0:T(8,128)(2,1)} %bitcast.31, bf16[7168,256]{1,0:T(8,128)(2,1)} %bitcast.22, bf16[7168,256]{1,0:T(8,128)(2,1)} %bitcast.24, bf16[7168,256]{1,0:T(8,128)(2,1)} %get-tuple-element.13.gb_ref, bf16[7168,256]{1,0:T(8,128)(2,1)} %get-tuple-element.14.ub_ref, ...), custom_call_target="tpu_custom_call" | custom-call | flops 22548578304 | bytes 51380224 | tf_op jit(solution)/shard_map/pallas_call | solution.py:310
  131.4 0.0 all-to-all-done
  131.4 80.4 %shard_map.88 = bf16[64,896]{1,0:T(8,128)(2,1)} custom-call(bf16[4,4,64,7168]{3,2,1,0:T(8,128)(2,1)} %bitcast.19), custom_call_target="tpu_custom_call" | custom-call | tf_op jit(solution)/shard_map/pallas_call | solution.py:580
  211.9 1.2 convolution_multiply_fusion
  213.1 1.6 copy.37
  (1 shorter events, 0.0 us)
Async XLA Ops:
  90.9 40.5 %all-to-all-start = ((bf16[8,64,1024]{2,1,0:T(8,128)(2,1)}), bf16[8,64,1024]{2,1,0:T(8,128)(2,1)S(1)}, u32[]{:S(2)}, u32[]{:S(2)}) async-start(bf16[8,64,1024]{2,1,0:T(8,128)(2,1)} %copy.33), calls=%async_computation | async-start | bytes 2097152 | tf_op jit(solution)/shard_map/all_to_all | solution.py:622

commit v6 on v5

--- a/solution.py
+++ b/solution.py
@@ -14,6 +14,8 @@
 SWAP_UNITS = 18
 PARTS = 2
 BANDS = ((0, 48), (48, 16))
+GATHER_ORDER = "1313210121032331010211332223322001203000"
+SCATTER_ORDER = "014S1011042414000222210230T11102225330412553435534554545333435"
 MESH = pl.DeviceIdType.MESH
 BF16 = jnp.bfloat16
 F32 = jnp.float32
@@ -79,7 +81,7 @@
 def gather_kernel(
     tok_ref, share_ref, wg_ref, wu_ref, wd_ref,
     all_ref, shares_ref, wg2_ref, wu2_ref, wd2_ref,
-    held, flow_send, flow_recv, z_send, z_recv, s_send, s_recv, w_send, w_recv, flush_sem,
+    flow_send, flow_recv, z_send, z_recv, s_send, s_recv, w_send, w_recv, local_sem,
 ):
     here = Place()
     rows, width = tok_ref.shape
@@ -109,8 +111,8 @@
 
         def send(t, rel, cols, along, step, local=False):
             block = here.block(axis, *rel)
-            src = tok_ref.at[band, cols] if local else held.at[block, band, cols]
-            return go(remote(src, held.at[block, band, cols], flow_send.at[number, t],
+            src = tok_ref.at[band, cols] if local else all_ref.at[block, band, cols]
+            return go(remote(src, all_ref.at[block, band, cols], flow_send.at[number, t],
                              flow_recv.at[number, t], here.toward(along, step)))
 
         def across(rel, which):
@@ -120,7 +122,7 @@
             slot = (rel[0] % SIDE) * SIDE + rel[1] % SIDE
             for side in which:
                 cols = (part_a, part_b)[side]
-                ref = held.at[block, band, cols]
+                ref = all_ref.at[block, band, cols]
                 part = number // 2
                 go(remote(ref, ref, z_send.at[part, side, slot], z_recv.at[part, side, slot],
                           here.device(dz=z_steps[side])))
@@ -190,8 +192,9 @@
         yield
 
     def extras():
-        yield
-        held[own] = tok_ref[...]
+        mine = pltpu.make_async_copy(tok_ref, all_ref.at[own], local_sem)
+        mine.start()
+        yield
         gifts = []
         for n, (i, j) in enumerate(offsets):
             gifts.append(go(remote(share_ref.at[here.block("x", i, j)], shares_ref.at[own],
@@ -204,39 +207,31 @@
             yield
         for gift in gifts:
             gift.wait_recv()
+        mine.wait()
 
     fixed = 2 * swap
     flows = []
     for part in range(PARTS):
         flows.append(flow(2 * part, "x", "y", fixed, width - fixed, False))
         flows.append(flow(2 * part + 1, "y", "x", swap_from, swap, True))
-    take_turns(flows + [extras()])
-    flushes = []
-
-    def flush(start, span):
-        cols = pl.ds(start, span)
-        copy = pltpu.make_async_copy(
-            held.at[:, :, cols], all_ref.at[:, :, cols], flush_sem.at[len(flushes)])
-        copy.start()
-        flushes.append(copy)
-
-    flush(fixed, width - fixed)
-    flush(swap_from, swap)
+    flows.append(extras())
+    for n, turn in enumerate(GATHER_ORDER):
+        next(flows[int(turn)])
+        if n % 4 == 0 and 0 < n < 36:
+            next(flows[-1])
+    take_turns(flows[-1:])
     half = swap // 2
     for part in range(PARTS):
         band = pl.ds(part * (rows // PARTS), rows // PARTS)
         for side in (0, 1):
             cols = pl.ds(pl.multiple_of(wanted_from + side * half, unit), half)
             for i, j in offsets:
-                ref = held.at[here.block("y", i, j), band, cols]
+                ref = all_ref.at[here.block("y", i, j), band, cols]
                 slot = i * SIDE + j
                 remote(ref, ref, z_send.at[part, side, slot], z_recv.at[part, side, slot],
                        here.device(dz=z_steps[side])).wait_recv()
-    flush(wanted_from, swap)
     for copy in started:
         copy.wait_send()
-    for copy in flushes:
-        copy.wait()
 
 
 def gather_all(tokens, share, w_gate, w_up, w_down):
@@ -253,10 +248,9 @@
         in_specs=[vmem, vmem, hbm, hbm, hbm],
         out_specs=[hbm, vmem, hbm, hbm, hbm],
         scratch_shapes=[
-            pltpu.VMEM((CHIPS, rows, width), BF16),
             dma((2 * PARTS, 20)), dma((2 * PARTS, 20)),
             dma((PARTS, 2, CHIPS)), dma((PARTS, 2, CHIPS)),
-            dma((CHIPS - 1,)), dma((CHIPS - 1,)), dma((3,)), dma((3,)), dma((3,)),
+            dma((CHIPS - 1,)), dma((CHIPS - 1,)), dma((3,)), dma((3,)), dma(()),
         ],
         compiler_params=pltpu.CompilerParams(
             collective_id=0, has_side_effects=True, vmem_limit_bytes=60 * 2**20
@@ -517,45 +511,19 @@
         flows[name, part] = flow(3 * part + n, part, *axes[n], starts[n], layout[n],
                                  swaps[part] if n == 2 else None)
 
-    def advance(names, part, count):
-        for _ in range(count):
-            for name in names:
-                next(flows[name, part])
-
-    begin("a", 0)
-    begin("b", 0)
-    advance("ab", 0, 1)
-    swaps[0] = swap(0)
-    swaps[1] = swap(1)
-    begin("c", 0)
-    advance("ab", 0, 2)
-    advance("c", 0, 1)
-    advance("ab", 0, 2)
-    advance("c", 0, 2)
-    begin("a", 1)
-    begin("b", 1)
-    advance("ab", 1, 1)
-    advance("c", 0, 2)
-    advance("ab", 0, 3)
-    advance("ab", 1, 2)
-    advance("c", 0, 1)
-    begin("c", 1)
-    advance("c", 1, 1)
-    advance("ab", 1, 2)
-    advance("ab", 0, 1)
-    advance("c", 0, 2)
-    advance("c", 1, 4)
-    advance("ab", 0, 1)
-    advance("c", 0, 1)
-    advance("ab", 1, 3)
-    advance("c", 0, 1)
-    last = [spread(0)]
-    advance("c", 1, 3)
-    advance("ab", 1, 1)
-    advance("c", 1, 1)
-    advance("ab", 1, 1)
-    advance("c", 1, 1)
-    last.append(spread(1))
+    turns, last = {}, {}
+    for turn in SCATTER_ORDER:
+        if turn in "ST":
+            part = "ST".index(turn)
+            swaps[part] = swap(part)
+            continue
+        part, name = int(turn) // 3, "abc"[int(turn) % 3]
+        if (name, part) not in flows:
+            begin(name, part)
+        next(flows[name, part])
+        turns[part] = turns.get(part, 0) + 1
+        if turns[part] == 30:
+            last[part] = spread(part)
     for part in range(2):
         finish(part, last[part])
     for copy in started:

time: 216 us -> 198 us (0.917)
  Pallas kernels: 199 us -> 181 us
    pallas_call x1, Pallas kernels: 83.6 us -> 69.4 us  [gather_all(): pl.pallas_call(gather_kernel, out_shape=[jax.ShapeDtypeStruct((CHIPS, row...]
    pallas_call x1, Pallas kernels: 80.4 us -> 77.4 us  [scatter_all(): pl.pallas_call(functools.partial(scatter_kernel, layout), out_shape=jax.S...]
  transfers between devices with their start and end apart: 1 -> 1, of which waited for: 0 -> 0; matrix products, arithmetic and copies ran while one was open for 1% -> 1% of each run, Pallas kernels for 16% -> 17%
where the time goes in v6:
time: 198 us; the launch traced here: 197 us
  Pallas kernels  181 us (91%)
  local copies, waits for them, and re-layouts  7.25 us (4%)
  starting transfers between devices  3.8 us (2%)
  other arithmetic  3.14 us (2%)
    pallas_call x1, Pallas kernels, scatter_all(): pl.pallas_call(functools.partial(scatter_kernel, layout), out_shape=jax.S...  77.4 us
    pallas_call x1, Pallas kernels, gather_all(): pl.pallas_call(gather_kernel, out_shape=[jax.ShapeDtypeStruct((CHIPS, row...  69.4 us
    pallas_call x1, Pallas kernels, experts(): pl.pallas_call(functools.partial(experts_kernel, steps), grid=(2 * steps,...  34.5 us
  transfers between devices with their start and end apart: 1, of which 0 were waited for; matrix products, arithmetic and copies ran while one was open for 1% of the time, Pallas kernels for 17%

profile of v6, /device:TPU:8, one launch (start us, length us, event | category | flops | bytes accessed | tf_op | source)
XLA Modules:
  0.0 197.4 jit_solution(445593964413877894)
XLA Ops:
  0.6 0.7 convert_reduce_fusion
  1.3 0.7 multiply_divide_fusion
  2.0 0.7 select_reduce_fusion
  2.8 0.1 broadcast_in_dim.35
  2.8 0.7 slice.16
  3.6 1.3 copy.35
  4.9 0.1 pad_maximum_fusion
  5.1 0.6 broadcast_in_dim.36.share_ref
  5.7 69.4 %shard_map.86 = (bf16[16,64,7168]{2,1,0:T(8,128)(2,1)}, f32[16,8,128]{2,1,0:T(8,128)}, bf16[7168,256]{1,0:T(8,128)(2,1)}, bf16[7168,256]{1,0:T(8,128)(2,1)}, bf16[256,7168]{1,0:T(8,128)(2,1)}) custom-call(bf16[64,7168]{1,0:T(8,128)(2,1)} %tok_ref.1, f32[16,8,128]{2,1,0:T(8,128)} %broadcast_in_dim.36.share_ref, bf16[7168,256]{1,0:T(8,128)(2,1)} %bitcast.21, ...), custom_call_target="tpu_custom_call" | custom-call | tf_op jit(solution)/shard_map/pallas_call | solution.py:242
  75.1 1.5 copy.33
  76.7 3.8 %all-to-all-start = ((bf16[8,64,1024]{2,1,0:T(8,128)(2,1)}), bf16[8,64,1024]{2,1,0:T(8,128)(2,1)S(1)}, u32[]{:S(2)}, u32[]{:S(2)}) async-start(bf16[8,64,1024]{2,1,0:T(8,128)(2,1)} %copy.33), calls=%async_computation | async-start | bytes 2097152 | tf_op jit(solution)/shard_map/all_to_all | solution.py:590
  80.5 0.9 slice_reduce_fusion
  81.3 0.1 reshape_squeeze.3
  81.4 0.2 copy.32
  81.6 0.2 rev.3
  81.8 0.9 broadcast_select_fusion
  82.7 34.5 %shard_map.87 = bf16[1024,7168]{1,0:T(8,128)(2,1)} custom-call(bf16[1024,7168]{1,0:T(8,128)(2,1)} %bitcast.31, bf16[7168,256]{1,0:T(8,128)(2,1)} %bitcast.22, bf16[7168,256]{1,0:T(8,128)(2,1)} %bitcast.24, bf16[7168,256]{1,0:T(8,128)(2,1)} %get-tuple-element.13.gb_ref, bf16[7168,256]{1,0:T(8,128)(2,1)} %get-tuple-element.14.ub_ref, ...), custom_call_target="tpu_custom_call" | custom-call | flops 22548578304 | bytes 51380224 | tf_op jit(solution)/shard_map/pallas_call | solution.py:304
  117.2 0.0 all-to-all-done
  117.2 77.4 %shard_map.88 = bf16[64,896]{1,0:T(8,128)(2,1)} custom-call(bf16[4,4,64,7168]{3,2,1,0:T(8,128)(2,1)} %bitcast.19), custom_call_target="tpu_custom_call" | custom-call | tf_op jit(solution)/shard_map/pallas_call | solution.py:548
  194.6 1.2 convolution_multiply_fusion
  195.8 1.6 copy.37
  (1 shorter events, 0.0 us)
Async XLA Ops:
  76.7 40.6 %all-to-all-start = ((bf16[8,64,1024]{2,1,0:T(8,128)(2,1)}), bf16[8,64,1024]{2,1,0:T(8,128)(2,1)S(1)}, u32[]{:S(2)}, u32[]{:S(2)}) async-start(bf16[8,64,1024]{2,1,0:T(8,128)(2,1)} %copy.33), calls=%async_computation | async-start | bytes 2097152 | tf_op jit(solution)/shard_map/all_to_all | solution.py:590
